TPU v7x, 32 devices: a whole 2x2x4 slice. The times are simulated.
32 devices in a mesh: rep: 4 (over x, y), dp: 8 (over z, core).
Axes of the slice: x: 2, y: 2, z: 4, core: 2. Of those that a mesh axis runs over, the one named last changes fastest.
Arguments:
- x: bfloat16 [32, 2048, 640], P(('rep', 'dp')), parts along dimension 0
- dy: bfloat16 [32, 2048, 640], P(('rep', 'dp')), parts along dimension 0
- w_gate: bfloat16 [2, 640, 2048], replicated
- w_up: bfloat16 [2, 640, 2048], replicated
- w_down: bfloat16 [2, 2048, 640], replicated
- m_w_gate: float32 [2, 640, 2048], P(None, 'dp')
- m_w_up: float32 [2, 640, 2048], P(None, 'dp')
- m_w_down: float32 [2, 2048, 640], P(None, 'dp')
- v_w_gate: float32 [2, 640, 2048], P(None, 'dp')
- v_w_up: float32 [2, 640, 2048], P(None, 'dp')
- v_w_down: float32 [2, 2048, 640], P(None, 'dp')
Outputs:
- output 1: bfloat16 [8, 640, 2048], P('rep'), parts along dimension 0
- output 2: bfloat16 [8, 640, 2048], P('rep'), parts along dimension 0
- output 3: bfloat16 [8, 2048, 640], P('rep'), parts along dimension 0
- output 4: float32 [8, 640, 2048], P('rep', 'dp'), parts along dimension 0
- output 5: float32 [8, 640, 2048], P('rep', 'dp'), parts along dimension 0
- output 6: float32 [8, 2048, 640], P('rep', 'dp'), parts along dimension 0
- output 7: float32 [8, 640, 2048], P('rep', 'dp'), parts along dimension 0
- output 8: float32 [8, 640, 2048], P('rep', 'dp'), parts along dimension 0
- output 9: float32 [8, 2048, 640], P('rep', 'dp'), parts along dimension 0
There are 4 independent parts. A program takes and returns all parts, laid end to end along the dimension named above; an argument that names none is the same for every part.
All inputs are finite; a program needn't handle non-finite values.
Results may differ from a plain program's by a relative error of at most 0.022.
Values are sent between devices in bfloat16 or wider.
A program may use at most 2 GiB of HBM per device.

v0:
```python
import jax
import jax.numpy as jnp
from jax import lax

NAMES = ("w_gate", "w_up", "w_down")


def matmul(a, w):
    return jnp.dot(a, w, preferred_element_type=jnp.float32).astype(jnp.bfloat16)


def normed(h):
    wide = h.astype(jnp.float32)
    scale = lax.rsqrt(jnp.mean(wide**2, -1, keepdims=True) + 1e-6)
    return (wide * scale).astype(jnp.bfloat16)


def layer(h, w):
    a = normed(h)
    gate = jnp.dot(a, w["w_gate"], preferred_element_type=jnp.float32)
    up = jnp.dot(a, w["w_up"], preferred_element_type=jnp.float32)
    return h + matmul((jax.nn.silu(gate) * up).astype(jnp.bfloat16), w["w_down"])


def adamw(w, m, v, g):
    m = 0.9 * m + 0.1 * g
    v = 0.95 * v + 0.05 * g * g
    step = m * lax.rsqrt(v + 1e-8) + 0.1 * w
    return (w - 0.02 * step).astype(jnp.bfloat16), m, v


def clipped(gradients, sum_of_squares, count):
    factor = jnp.minimum(1.0, 0.5 * lax.rsqrt(sum_of_squares / count + 1e-30))
    return [g * factor for g in gradients]


def stack(weights, h):
    for number in range(weights["w_gate"].shape[0]):
        h = layer(h, {name: w[number] for name, w in weights.items()})
    return h


def solution(mesh):
    groups = mesh.shape["rep"]

    def step(x, dy, *arrays):
        weights, m, v = (arrays[i : i + 3] for i in (0, 3, 6))
        x, dy = (t.reshape(groups, -1, *t.shape[1:]) for t in (x, dy))

        def of_a_group(x, dy):
            _, back = jax.vjp(lambda w: stack(w, x), dict(zip(NAMES, weights, strict=True)))
            by_weights = back(dy)[0]
            gradients = [by_weights[name].astype(jnp.float32) for name in NAMES]
            gradients = clipped(gradients, sum(jnp.sum(g * g) for g in gradients), sum(g.size for g in gradients))
            new = [adamw(w.astype(jnp.float32), m, v, g) for w, m, v, g in zip(weights, m, v, gradients, strict=True)]
            return tuple(one[which] for which in range(3) for one in new)

        return tuple(t.reshape(-1, *t.shape[2:]) for t in jax.vmap(of_a_group)(x, dy))

    return step
```

profile of v0, /device:TPU:0, one launch (start us, length us, event | category | flops | bytes accessed | tf_op | source)
XLA Modules:
  0.0 678.8 jit_solution(16780096686600728704)
XLA Ops:
  14.1 8.6 %fusion.76 = f32[2048,2048]{1,0:T(8,128)S(1)} fusion(bf16[2,640,2048]{2,1,0:T(8,128)(2,1)} %param, bf16[1,2048,640]{2,1,0:T(8,128)(2,1)S(1)} %copy-done.1, f32[2048]{0:T(1024)S(1)} %add_rsqrt_fusion), kind=kOutput, calls=%fused_computation.88 | convolution fusion | flops 5372641280 | bytes 22028288 | tf_op jit(solution)/vmap(jvp())/dot_general | solution.py:20
  22.7 13.6 %fusion.74 = f32[2048,2048]{1,0:T(8,128)} fusion(bf16[2,640,2048]{2,1,0:T(8,128)(2,1)} %param.3, bf16[1,2048,640]{2,1,0:T(8,128)(2,1)S(1)} %copy-done.1, f32[2048]{0:T(1024)S(1)} %add_rsqrt_fusion), kind=kOutput, calls=%fused_computation.86 | convolution fusion | flops 5372641280 | bytes 22028288 | tf_op jit(solution)/vmap(jvp())/dot_general | solution.py:21
  36.3 8.6 %fusion.26 = bf16[2048,2048]{1,0:T(8,128)(2,1)S(1)} fusion(f32[2048,2048]{1,0:T(8,128)} %fusion.74, f32[2048,2048]{1,0:T(8,128)S(1)} %fusion.76), kind=kLoop, calls=%fused_computation.39 | loop fusion | flops 25165824 | bytes 41943040
  44.9 10.1 %fusion.39 = (f32[2048]{0:T(1024)S(1)}, bf16[1,1,2048,640]{2,3,1,0:T(8,128)(2,1)S(1)}) fusion(bf16[2048,2048]{1,0:T(8,128)(2,1)S(1)} %fusion.26, bf16[2,2048,640]{2,1,0:T(8,128)(2,1)} %param.4, bf16[1,2048,640]{1,2,0:T(8,128)(2,1)S(1)} %copy-done.11), kind=kOutput, calls=%fused_computation.56 | convolution fusion | flops 5375260672 | bytes 16261120 | tf_op jit(solution)/vmap(jvp())/dot_general | solution.py:9
  55.1 12.9 %fusion.63 = f32[2048,2048]{1,0:T(8,128)} fusion(bf16[2,640,2048]{2,1,0:T(8,128)(2,1)} %param, bf16[1,1,2048,640]{2,3,1,0:T(8,128)(2,1)S(1)} %get-tuple-element.10, f32[2048]{0:T(1024)S(1)} %bitcast.347), kind=kOutput, calls=%fused_computation.75 | convolution fusion | flops 5372641280 | bytes 22028288 | tf_op jit(solution)/vmap(jvp())/dot_general | solution.py:20
  67.9 12.1 %fusion.66 = f32[2048,2048]{1,0:T(8,128)} fusion(bf16[2,640,2048]{2,1,0:T(8,128)(2,1)} %param.3, bf16[1,1,2048,640]{2,3,1,0:T(8,128)(2,1)S(1)} %get-tuple-element.10, f32[2048]{0:T(1024)S(1)} %bitcast.348), kind=kOutput, calls=%fused_computation.78 | convolution fusion | flops 5372641280 | bytes 22028288 | tf_op jit(solution)/vmap(jvp())/dot_general | solution.py:21
  80.1 16.1 %fusion.42 = f32[1,2048,640]{2,1,0:T(8,128)} fusion(f32[2048,2048]{1,0:T(8,128)} %fusion.66, f32[2048,2048]{1,0:T(8,128)} %fusion.63, bf16[1,2048,640]{2,1,0:T(8,128)(2,1)S(1)} %copy-done.10), kind=kOutput, calls=%fused_computation.61 | convolution fusion | flops 5393874944 | bytes 41418752 | tf_op jit(solution)/vmap(transpose(jvp()))/dot_general | solution.py:9
  96.2 9.4 %convolution_convert_fusion.1 = bf16[2048,2048]{1,0:T(8,128)(2,1)S(1)} fusion(bf16[1,2048,640]{2,1,0:T(8,128)(2,1)S(1)} %copy-done.10, bf16[2,2048,640]{2,1,0:T(8,128)(2,1)} %param.4), kind=kOutput, calls=%fused_computation.48 | convolution fusion | flops 5372903424 | bytes 13631488 | tf_op jit(solution)/vmap(transpose(jvp()))/dot_general | solution.py:9
  108.8 15.8 %fusion.6 = bf16[2048,2048]{1,0:T(8,128)(2,1)} fusion(f32[2048,2048]{1,0:T(8,128)} %fusion.63, f32[2048,2048]{1,0:T(8,128)} %fusion.66, bf16[2048,2048]{1,0:T(8,128)(2,1)S(1)} %convolution_convert_fusion.1), kind=kLoop, calls=%fused_computation.11 | loop fusion | flops 50331648 | bytes 50331648
  127.7 13.2 %fusion.54 = bf16[2048,640]{0,1:T(8,128)(2,1)} fusion(bf16[2048,2048]{1,0:T(8,128)(2,1)} %copy-done.4, f32[2048,2048]{1,0:T(8,128)} %fusion.63, bf16[2,640,2048]{2,1,0:T(8,128)(2,1)} %param.3), kind=kOutput, calls=%fused_computation.66 | convolution fusion | flops 5395185664 | bytes 30408704 | tf_op jit(solution)/vmap(transpose(jvp()))/dot_general | solution.py:21
  152.5 11.0 %convolution_bitcast_fusion.1 = f32[1,2048,640]{2,1,0:T(8,128)} fusion(bf16[2048,2048]{1,0:T(8,128)(2,1)} %copy-done.2, bf16[2048,640]{0,1:T(8,128)(2,1)S(1)} %fusion.61), kind=kOutput, calls=%fused_computation.65 | convolution fusion | flops 5368709120 | bytes 16252928 | tf_op jit(solution)/vmap(transpose(jvp()))/dot_general | solution.py:9
  165.2 12.9 %fusion.45 = f32[1,640,2048]{2,1,0:T(8,128)} fusion(bf16[2048,2048]{1,0:T(8,128)(2,1)} %copy-done.4, f32[2048,2048]{1,0:T(8,128)} %fusion.63, bf16[1,1,2048,640]{2,3,1,0:T(8,128)(2,1)S(1)} %copy-done.8, f32[2048]{0:T(1024)S(1)} %bitcast.350), kind=kOutput, calls=%fused_computation.62 | convolution fusion | flops 5397807104 | bytes 33038336 | tf_op jit(solution)/vmap(transpose(jvp()))/dot_general | solution.py:21
  178.2 9.5 %convolution_convert_fusion = bf16[2048,2048]{1,0:T(8,128)(2,1)S(1)} fusion(bf16[2048,640]{0,1:T(8,128)(2,1)} %copy-done.9, bf16[2,2048,640]{2,1,0:T(8,128)(2,1)} %param.4), kind=kOutput, calls=%fused_computation.47 | convolution fusion | flops 5372903424 | bytes 13631488 | tf_op jit(solution)/vmap(transpose(jvp()))/dot_general | solution.py:9
  190.9 11.3 %fusion.51 = f32[1,640,2048]{2,1,0:T(8,128)} fusion(bf16[2048,2048]{1,0:T(8,128)(2,1)S(1)} %convolution_convert_fusion, f32[2048,2048]{1,0:T(8,128)} %copy-done, bf16[1,2048,640]{1,2,0:T(8,128)(2,1)S(1)} %copy-done.12, f32[2048]{0:T(1024)S(1)} %copy-done.17), kind=kOutput, calls=%fused_computation.64 | convolution fusion | flops 5397807104 | bytes 33038336 | tf_op jit(solution)/vmap(transpose(jvp()))/dot_general | solution.py:21
  202.3 9.4 %convolution_bitcast_fusion = f32[1,640,2048]{2,1,0:T(8,128)} fusion(bf16[2048,2048]{1,0:T(8,128)(2,1)} %fusion.6, bf16[1,1,2048,640]{2,3,1,0:T(8,128)(2,1)S(1)} %copy-done.8, f32[2048]{0:T(1024)S(1)} %bitcast.351), kind=kOutput, calls=%fused_computation.60 | convolution fusion | flops 5372641280 | bytes 16261120 | tf_op jit(solution)/vmap(transpose(jvp()))/dot_general | solution.py:20
  213.5 20.1 %fusion.48 = f32[1,640,2048]{2,1,0:T(8,128)} fusion(f32[2048,2048]{1,0:T(8,128)} %copy-done, f32[2048,2048]{1,0:T(8,128)} %fusion.74, bf16[2048,2048]{1,0:T(8,128)(2,1)} %copy-done.19, bf16[1,2048,640]{1,2,0:T(8,128)(2,1)S(1)} %copy-done.13, f32[2048]{0:T(1024)S(1)} %copy-done.17), kind=kOutput, calls=%fused_computation.63 | convolution fusion | flops 5418778624 | bytes 49815552 | tf_op jit(solution)/vmap(transpose(jvp()))/dot_general | solution.py:20
  238.8 48.0 %reduce-scatter.23.cloned.1.call-done = f32[1,80,2048]{2,1,0:T(8,128)} async-done(((f32[1,640,2048]{2,1,0:T(8,128)}), f32[1,80,2048]{2,1,0:T(8,128)}) %reduce-scatter.23.cloned.1.call-update) | async-done | bytes 655376
  288.0 60.2 %reduce-scatter.25.cloned.1.call-done = f32[1,80,2048]{2,1,0:T(8,128)} async-done(((f32[1,640,2048]{2,1,0:T(8,128)}), f32[1,80,2048]{2,1,0:T(8,128)}) %reduce-scatter.25.cloned.1.call-update) | async-done | bytes 655376
  350.2 59.2 %reduce-scatter.19.cloned.1.call-done = f32[1,80,2048]{2,1,0:T(8,128)} async-done(((f32[1,640,2048]{2,1,0:T(8,128)}), f32[1,80,2048]{2,1,0:T(8,128)}) %reduce-scatter.19.cloned.1.call-update) | async-done | bytes 655376
  410.5 60.1 %reduce-scatter.21.cloned.1.call-done = f32[1,80,2048]{2,1,0:T(8,128)} async-done(((f32[1,640,2048]{2,1,0:T(8,128)}), f32[1,80,2048]{2,1,0:T(8,128)}) %reduce-scatter.21.cloned.1.call-update) | async-done | bytes 655376
  474.7 14.9 %all-reduce.16 = f32[1]{0:T(128)} all-reduce(f32[1]{0:T(128)} %bitcast.50), channel_id=5, replica_groups=mesh['rep'=4,'dp'=8] {'dp'}, use_global_device_ids=true, to_apply=%region_3.4.clone | all-reduce | flops 1 | bytes 8 | tf_op jit(solution)/vmap()/reduce_sum | solution.py:54
  502.8 45.3 %all-gather.14.cloned.1.call-done = bf16[1,2,2048,640]{3,2,1,0:T(8,128)(2,1)} async-done(((bf16[1,2,256,640]{3,2,1,0:T(8,128)(2,1)}), bf16[1,2,2048,640]{3,2,1,0:T(8,128)(2,1)}) %all-gather.14.cloned.1.call-update) | async-done | bytes 5242896 | tf_op jit(solution)/reshape | solution.py:58
  548.1 56.4 %all-gather.10.cloned.1.call-done = bf16[1,2,640,2048]{3,2,1,0:T(8,128)(2,1)} async-done(((bf16[1,2,80,2048]{3,2,1,0:T(8,128)(2,1)}), bf16[1,2,640,2048]{3,2,1,0:T(8,128)(2,1)}) %all-gather.10.cloned.1.call-update) | async-done | bytes 5242896 | tf_op jit(solution)/reshape | solution.py:58
  604.5 56.4 %all-gather.12.cloned.1.call-done = bf16[1,2,640,2048]{3,2,1,0:T(8,128)(2,1)} async-done(((bf16[1,2,80,2048]{3,2,1,0:T(8,128)(2,1)}), bf16[1,2,640,2048]{3,2,1,0:T(8,128)(2,1)}) %all-gather.12.cloned.1.call-update) | async-done | bytes 5242896 | tf_op jit(solution)/reshape | solution.py:58
  (90 shorter events, 65.7 us)
Async XLA Ops:
  7.2 6.9 %copy-start.1 = (bf16[1,2048,640]{2,1,0:T(8,128)(2,1)S(1)}, bf16[1,2048,640]{2,1,0:T(8,128)(2,1)}, u32[]{:S(2)}) copy-start(bf16[1,2048,640]{2,1,0:T(8,128)(2,1)} %param.2) | copy-start | bytes 7864324
  7.2 228.4 %reduce-scatter.27.cloned.1.call-start = ((), (), s32[]{:S(2)}) async-start(), calls=%async_computation.13 | async-start | bytes 5898240
  14.1 8.6 %copy-start.16 = (f32[2048]{0:T(1024)}, f32[2048]{0:T(1024)S(1)}, u32[]{:S(2)}) copy-start(f32[2048]{0:T(1024)S(1)} %add_rsqrt_fusion) | copy-start | bytes 24580
  22.7 13.6 %copy-start = (f32[2048,2048]{1,0:T(8,128)}, f32[2048,2048]{1,0:T(8,128)S(1)}, u32[]{:S(2)}) copy-start(f32[2048,2048]{1,0:T(8,128)S(1)} %fusion.76) | copy-start | bytes 50331652
  36.3 8.6 %copy-start.11 = (bf16[1,2048,640]{1,2,0:T(8,128)(2,1)S(1)}, bf16[1,2048,640]{1,2,0:T(8,128)(2,1)}, u32[]{:S(2)}) copy-start(bf16[1,2048,640]{1,2,0:T(8,128)(2,1)} %copy) | copy-start | bytes 7864324
  44.9 10.1 %copy-start.2 = (bf16[2048,2048]{1,0:T(8,128)(2,1)}, bf16[2048,2048]{1,0:T(8,128)(2,1)S(1)}, u32[]{:S(2)}) copy-start(bf16[2048,2048]{1,0:T(8,128)(2,1)S(1)} %fusion.26) | copy-start | bytes 25165828
  55.0 12.9 %copy-start.6 = (bf16[1,1,2048,640]{2,3,1,0:T(8,128)(2,1)}, bf16[1,1,2048,640]{2,3,1,0:T(8,128)(2,1)S(1)}, u32[]{:S(2)}) copy-start(bf16[1,1,2048,640]{2,3,1,0:T(8,128)(2,1)S(1)} %get-tuple-element.10) | copy-start | bytes 7864324
  67.9 12.1 %copy-start.10 = (bf16[1,2048,640]{2,1,0:T(8,128)(2,1)S(1)}, bf16[1,2048,640]{2,1,0:T(8,128)(2,1)}, u32[]{:S(2)}) copy-start(bf16[1,2048,640]{2,1,0:T(8,128)(2,1)} %param.5) | copy-start | bytes 7864324
  96.2 140.5 %reduce-scatter.29.cloned.1.call-start = ((), (), s32[]{:S(2)}) async-start(), calls=%async_computation.14 | async-start | bytes 5898240
  127.6 13.3 %copy-start.3 = (bf16[2048,2048]{1,0:T(8,128)(2,1)S(1)}, bf16[2048,2048]{1,0:T(8,128)(2,1)}, u32[]{:S(2)}) copy-start(bf16[2048,2048]{1,0:T(8,128)(2,1)} %fusion.6) | copy-start | bytes 25165828
  127.7 13.2 %copy-start.7 = (bf16[1,1,2048,640]{2,3,1,0:T(8,128)(2,1)S(1)}, bf16[1,1,2048,640]{2,3,1,0:T(8,128)(2,1)}, u32[]{:S(2)}) copy-start(bf16[1,1,2048,640]{2,3,1,0:T(8,128)(2,1)} %copy-done.6) | copy-start | bytes 7864324
  163.5 123.4 %reduce-scatter.23.cloned.1.call-start = ((), (), s32[]{:S(2)}) async-start(), calls=%async_computation.11 | async-start | bytes 5898240
  178.1 12.8 %copy-start.17 = (f32[2048]{0:T(1024)S(1)}, f32[2048]{0:T(1024)}, u32[]{:S(2)}) copy-start(f32[2048]{0:T(1024)} %copy-done.16) | copy-start | bytes 24580
  178.1 170.0 %reduce-scatter.25.cloned.1.call-start = ((), (), s32[]{:S(2)}) async-start(), calls=%async_computation.12 | async-start | bytes 5898240
  178.2 12.8 %copy-start.12 = (bf16[1,2048,640]{1,2,0:T(8,128)(2,1)S(1)}, bf16[1,2048,640]{1,2,0:T(8,128)(2,1)}, u32[]{:S(2)}) copy-start(bf16[1,2048,640]{1,2,0:T(8,128)(2,1)} %copy) | copy-start | bytes 7864324
  202.3 207.1 %reduce-scatter.19.cloned.1.call-start = ((), (), s32[]{:S(2)}) async-start(), calls=%async_computation.9 | async-start | bytes 5898240
  211.8 258.9 %reduce-scatter.21.cloned.1.call-start = ((), (), s32[]{:S(2)}) async-start(), calls=%async_computation.10 | async-start | bytes 5898240
  233.7 256.6 %copy-start.14 = (f32[2,256,640]{2,1,0:T(8,128)S(1)}, f32[2,256,640]{2,1,0:T(8,128)}, u32[]{:S(2)}) copy-start(f32[2,256,640]{2,1,0:T(8,128)} %param.10) | copy-start | bytes 3932164
  233.7 314.4 %all-gather.14.cloned.1.call-start = ((), (), s32[]{:S(2)}) async-start(), calls=%async_computation.8 | async-start | bytes 5898240 | tf_op jit(solution)/reshape | solution.py:58
  494.2 4.6 copy-start.15
  494.3 110.2 %all-gather.10.cloned.1.call-start = ((), (), s32[]{:S(2)}) async-start(), calls=%async_computation.6 | async-start | bytes 5898240 | tf_op jit(solution)/reshape | solution.py:58
  498.8 162.2 %all-gather.12.cloned.1.call-start = ((), (), s32[]{:S(2)}) async-start(), calls=%async_computation.7 | async-start | bytes 5898240 | tf_op jit(solution)/reshape | solution.py:58
  661.0 6.2 copy-start.5
  661.0 8.5 %slice-start = ((s8[5242880]{0:T(1024)(128)(4,1)}), s8[4194304]{0:T(1024)(128)(4,1)S(1)}, s32[]{:S(2)}) async-start(s8[5242880]{0:T(1024)(128)(4,1)} %bitcast.339), calls=%async_computation.15 | async-start | bytes 8388608
  (7 other events, 14.5 us)
Sparse Core Ops, SparseCore 0:
  96.3 62.3 reduce-scatter.26
  163.6 62.3 reduce-scatter.28
  228.3 58.4 reduce-scatter.22
  289.6 58.5 reduce-scatter.24
  350.9 58.4 reduce-scatter.18
  412.1 58.4 reduce-scatter.20
  494.4 53.6 all-gather.13
  550.3 54.2 all-gather.9
  606.7 54.2 all-gather.11
where the time goes:
time: 688 us; the launch traced here: 679 us
  waiting for transfers between devices  386 us (56%)
  matrix products  178 us (26%)
  other arithmetic  50.6 us (7%)
  local copies, waits for them, and re-layouts  30.7 us (4%)
  between operations  17.9 us (3%)
  blocking collectives  14.9 us (2%)
    unnamed x15, waiting for transfers between devices  228 us
    reshape x3, waiting for transfers between devices, step(): t.reshape(-1, *t.shape[2:])  158 us
    dot_general x5, matrix products, layer(): up = jnp.dot(a, w['w_up'], preferred_element_type=jnp.float32)  63.1 us
    dot_general x5, matrix products, layer(): gate = jnp.dot(a, w['w_gate'], preferred_element_type=jnp.float32)  59.2 us
    dot_general x5, matrix products, matmul(): jnp.dot(a, w, preferred_element_type=jnp.float32).astype(jnp.bfloat16)  56 us
    unnamed x49, local copies, waits for them, and re-layouts  30.1 us
    unnamed x4, other arithmetic  26.2 us
    reduce_sum x1, blocking collectives, of_a_group(): jnp.sum(g * g)  14.9 us
  transfers between devices with their start and end apart: 9, of which 7 were waited for; matrix products, arithmetic and copies ran while one was open for 21% of the time, Pallas kernels for 0%

commit v1 on v0

v1 whole, which is shorter than its diff:
```python
import functools

import jax
import jax.numpy as jnp
from jax import lax
from jax.experimental import pallas as pl
from jax.experimental.pallas import tpu as pltpu
from jax.sharding import PartitionSpec as P

NAMES = ("w_gate", "w_up", "w_down")
MESH = pl.DeviceIdType.MESH
F32, BF16 = jnp.float32, jnp.bfloat16
ORDER = ((1, 2), (1, 0), (1, 1), (0, 2), (0, 0), (0, 1))
N = len(ORDER)


def chunks(rows, body):
    @pl.loop(0, rows // 16)
    def _(t):
        body(pl.ds(pl.multiple_of(t * 16, 16), 16))


def comm_kernel(count, *refs):
    grads, refs = refs[:N], refs[N:]
    w_in, m_in, v_in, refs = refs[:3], refs[3:6], refs[6:9], refs[9:]
    full, m_out, v_out, refs = refs[:3], refs[3:6], refs[6:9], refs[9:]
    xs, rs, olds, refs = refs[:3], refs[3:6], refs[6:9], refs[9:]
    squares, norms, fill_sem, load_sem, x_send, x_recv, r_send, r_recv, n_send, n_recv, g_send, g_recv = refs

    rep, me = lax.axis_index("rep"), lax.axis_index("dp")
    z, k = me // 2, lax.rem(me, 2)
    flip = z >= 2
    inner = jnp.logical_or(z == 1, z == 2)
    outer = jnp.logical_not(inner)

    def blk(mirrored):
        return jnp.where(flip, 3 - mirrored, mirrored)

    own = jnp.where(inner, blk(1), blk(0))
    ahead = jnp.where(flip, z - 1, z + 1)
    back = jnp.where(outer, z, jnp.where(flip, z + 1, z - 1))

    def device(zz, kk):
        return (rep, 2 * zz + kk)

    def remote(src, dst, send, recv, to):
        return pltpu.make_async_remote_copy(
            src_ref=src, dst_ref=dst, send_sem=send, recv_sem=recv, device_id=to, device_id_type=MESH
        )

    def load(i):
        layer, which = ORDER[i]
        rows = m_in[which].shape[1]
        return (
            pltpu.make_async_copy(m_in[which].at[layer], m_out[which].at[layer], load_sem.at[i, 0]),
            pltpu.make_async_copy(v_in[which].at[layer], v_out[which].at[layer], load_sem.at[i, 1]),
            pltpu.make_async_copy(
                w_in[which].at[layer, pl.ds(pl.multiple_of(me * rows, 16), rows)], olds[which].at[layer], load_sem.at[i, 2]
            ),
        )

    def fill(i):
        layer, which = ORDER[i]
        return pltpu.make_async_copy(grads[i], full[which].at[layer], fill_sem.at[i])

    def exchange(i):
        layer, which = ORDER[i]
        return remote(full[which].at[layer, :, 1 - k], xs[which].at[layer], x_send.at[i], x_recv.at[i], device(z, 1 - k))

    def hop(i, block, slot, send, to):
        layer, which = ORDER[i]
        return remote(
            full[which].at[layer, block, k], rs[which].at[layer, slot], r_send.at[i, send], r_recv.at[i, slot], device(to, k)
        )

    def add(i, block, slots):
        layer, which = ORDER[i]
        mine, x, r = full[which].at[layer, block, k], xs[which].at[layer, block], rs[which].at[layer]

        def body(at):
            total = mine[at, :].astype(F32) + x[at, :].astype(F32)
            for slot in slots:
                total += r[slot, at, :].astype(F32)
            mine[at, :] = total.astype(BF16)

        chunks(mine.shape[0], body)

    def finish(i):
        layer, which = ORDER[i]
        mine = full[which].at[layer, own, k]

        @pl.when(outer)
        def _():
            hop(i, blk(0), 0, 0, ahead).wait_recv()
            add(i, own, (0,))

        @pl.when(inner)
        def _():
            hop(i, blk(1), 2, 2, ahead).wait_recv()
            hop(i, blk(1), 4, 2, ahead).wait_recv()
            add(i, own, (2, 4))

        def body(at):
            g = mine[at, :].astype(F32)
            g = g * g
            total = squares[...]
            for c in range(g.shape[1] // 128):
                total += g[:8, c * 128 : (c + 1) * 128] + g[8:, c * 128 : (c + 1) * 128]
            squares[...] = total

        chunks(mine.shape[0], body)

    for i in range(N):
        fill(i).start()
    squares[...] = jnp.zeros_like(squares)

    barrier = pltpu.get_barrier_semaphore()
    for p in range(1, 8):
        pl.semaphore_signal(barrier, inc=1, device_id=(rep, lax.rem(me + p, 8)), device_id_type=MESH)
    pl.semaphore_wait(barrier, 7)

    for i in range(N):
        fill(i).wait()
        exchange(i).start()
    for i in range(N):
        for copy in load(i):
            copy.start()

    for i in range(N):
        exchange(i).wait_recv()

        @pl.when(outer)
        def _():
            for j in range(3):
                add(i, blk(3 - j), ())
                hop(i, blk(3 - j), j, j, ahead).start()

        @pl.when(inner)
        def _():
            hop(i, blk(3), 0, 0, ahead).wait_recv()
            add(i, blk(3), (0,))
            hop(i, blk(3), 3, 0, ahead).start()
            hop(i, blk(2), 1, 1, ahead).wait_recv()
            add(i, blk(2), (1,))
            hop(i, blk(2), 4, 1, ahead).start()
            hop(i, blk(0), 3, 2, ahead).wait_recv()
            add(i, blk(0), (3,))
            hop(i, blk(0), 0, 2, back).start()

        if i >= 1:
            finish(i - 1)
    finish(N - 1)
    for i in range(N):
        exchange(i).wait_send()
        for j in range(3):
            hop(i, blk(0), 0, j, ahead).wait_send()

    norms[me] = squares[...]

    def norm(p, src):
        return remote(norms.at[src], norms.at[src], n_send.at[p - 1], n_recv.at[src], (rep, lax.rem(me + p, 8)))

    for p in range(1, 8):
        norm(p, me).start()
    for p in range(1, 8):
        norm(p, lax.rem(me + p, 8)).wait_recv()
    total = norms[0]
    for d in range(1, 8):
        total += norms[d]
    ss = jnp.sum(total, keepdims=True)
    factor = jnp.minimum(1.0, 0.5 * lax.rsqrt(ss / count + 1e-30))

    def update(i):
        layer, which = ORDER[i]
        for copy in load(i):
            copy.wait()
        mine, m, v, w = full[which].at[layer, own, k], m_out[which].at[layer], v_out[which].at[layer], olds[which].at[layer]

        def body(at):
            g = mine[at, :].astype(F32) * factor
            new_m = 0.9 * m[at, :] + 0.1 * g
            new_v = 0.95 * v[at, :] + 0.05 * g * g
            old = w[at, :].astype(F32)
            step = new_m * lax.rsqrt(new_v + 1e-8) + 0.1 * old
            m[at, :] = new_m
            v[at, :] = new_v
            mine[at, :] = (old - 0.02 * step).astype(BF16)

        chunks(mine.shape[0], body)

    def pass_on(i, block, which_way, to, plane):
        layer, which = ORDER[i]
        here = full[which].at[layer, block, plane]
        return remote(here, here, g_send.at[i, block, which_way], g_recv.at[i, block, plane], to)

    def ahead_copy(i, block):
        return pass_on(i, block, 0, device(ahead, k), k)

    def back_copy(i, block):
        return pass_on(i, block, 1, device(back, k), k)

    def across_copy(i, block):
        return pass_on(i, block, 2, device(z, 1 - k), k)

    for s in range(N + 3):
        if s < N:
            update(s)

            @pl.when(inner)
            def _():
                back_copy(s, own).start()

            ahead_copy(s, own).start()
            across_copy(s, own).start()
        if 0 <= s - 1 < N:
            i = s - 1

            @pl.when(outer)
            def _():
                ahead_copy(i, blk(1)).wait_recv()
                across_copy(i, blk(1)).start()

            @pl.when(inner)
            def _():
                ahead_copy(i, blk(2)).wait_recv()
                back_copy(i, blk(2)).start()
                across_copy(i, blk(2)).start()
                ahead_copy(i, blk(0)).wait_recv()
                ahead_copy(i, blk(0)).start()
                across_copy(i, blk(0)).start()

        if 0 <= s - 2 < N:
            i = s - 2

            @pl.when(outer)
            def _():
                ahead_copy(i, blk(2)).wait_recv()
                across_copy(i, blk(2)).start()

            @pl.when(inner)
            def _():
                ahead_copy(i, blk(3)).wait_recv()
                back_copy(i, blk(3)).start()
                across_copy(i, blk(3)).start()

        if 0 <= s - 3 < N:
            i = s - 3

            @pl.when(outer)
            def _():
                ahead_copy(i, blk(3)).wait_recv()
                across_copy(i, blk(3)).start()

    for p in range(1, 8):
        norm(p, me).wait_send()
    for i in range(N):
        for b in range(4):
            pass_on(i, b, 2, device(z, 1 - k), 1 - k).wait_recv()
            across_copy(i, b).wait_send()
        ahead_copy(i, own).wait_send()

        @pl.when(inner)
        def _():
            ahead_copy(i, blk(0)).wait_send()
            for b in range(1, 4):
                back_copy(i, blk(b)).wait_send()


def shapes_of(w):
    layers, rows, columns = w.shape
    return layers, rows // 8, columns


def exchange_and_update(grads, weights, ms, vs):
    dims = [shapes_of(w) for w in weights]
    count = float(sum(w.size for w in weights))
    any_space = pl.BlockSpec(memory_space=pl.ANY)
    vmem = pl.BlockSpec(memory_space=pltpu.VMEM)
    grads = [grads[layer][which] for layer, which in ORDER]
    grads = [g.reshape(4, 2, g.shape[0] // 8, g.shape[1]) for g in grads]
    dma = pltpu.SemaphoreType.DMA
    out = pl.pallas_call(
        functools.partial(comm_kernel, count),
        out_shape=[jax.ShapeDtypeStruct((l, 4, 2, r, c), BF16) for l, r, c in dims]
        + [jax.ShapeDtypeStruct(d, F32) for d in dims] * 2,
        in_specs=[any_space] * (N + 9),
        out_specs=[vmem] * 9,
        scratch_shapes=[pltpu.VMEM((l, 4, r, c), BF16) for l, r, c in dims]
        + [pltpu.VMEM((l, 5, r, c), BF16) for l, r, c in dims]
        + [pltpu.VMEM(d, BF16) for d in dims]
        + [
            pltpu.VMEM((8, 128), F32),
            pltpu.VMEM((8, 8, 128), F32),
            dma((N,)),
            dma((N, 3)),
            dma((N,)),
            dma((N,)),
            dma((N, 3)),
            dma((N, 5)),
            dma((7,)),
            dma((8,)),
            dma((N, 4, 3)),
            dma((N, 4, 2)),
        ],
        compiler_params=pltpu.CompilerParams(collective_id=0, has_side_effects=True, vmem_limit_bytes=60 * 2**20),
        name="reduce_step_gather",
    )(*grads, *weights, *ms, *vs)
    new_w = [o.reshape(w.shape) for o, w in zip(out[:3], weights)]
    return (*new_w, *out[3:])


def matmul(a, w):
    return jnp.dot(a, w, preferred_element_type=jnp.float32).astype(jnp.bfloat16)


def normed(h):
    wide = h.astype(jnp.float32)
    scale = lax.rsqrt(jnp.mean(wide**2, -1, keepdims=True) + 1e-6)
    return (wide * scale).astype(jnp.bfloat16)


def layer(h, w):
    a = normed(h)
    gate = jnp.dot(a, w[0], preferred_element_type=jnp.float32)
    up = jnp.dot(a, w[1], preferred_element_type=jnp.float32)
    return h + matmul((jax.nn.silu(gate) * up).astype(jnp.bfloat16), w[2])


def stack(weights, h):
    for w in weights:
        h = layer(h, w)
    return h


def gradients(x, dy, weights):
    each = [[w[number] for w in weights] for number in range(2)]
    return jax.vjp(lambda w: stack(w, x), each)[1](dy)[0]


def solution(mesh):
    def step(x, dy, *arrays):
        weights, ms, vs = (arrays[i : i + 3] for i in (0, 3, 6))
        return exchange_and_update(gradients(x[0], dy[0], weights), weights, ms, vs)

    every, rows, whole = P(("rep", "dp")), P(None, "dp"), P(None)
    return jax.shard_map(
        step,
        mesh=mesh,
        in_specs=(every, every, whole, whole, whole) + (rows,) * 6,
        out_specs=(P("rep"),) * 3 + (P("rep", "dp"),) * 6,
        check_vma=False,
    )
```

time: 688 us -> 523 us (0.76)
  waiting for transfers between devices: 386 us -> 0 us
  Pallas kernels: 0 us -> 283 us
  other arithmetic: 50.6 us -> 4.97 us
  matrix products: 178 us -> 203 us
  between operations: 17.9 us -> 1.29 us
  blocking collectives: 14.9 us -> 0 us
  local copies, waits for them, and re-layouts: 30.7 us -> 23.6 us
    pallas_call x0 -> x1, Pallas kernels: none -> 283 us  [exchange_and_update(): pl.pallas_call(functools.partial(comm_kernel, count), out_shape=[jax.Shap...]
    unnamed x15 -> x0, waiting for transfers between devices: 228 us -> none
    reshape x3 -> x0, waiting for transfers between devices: 158 us -> none  [step(): t.reshape(-1, *t.shape[2:])]
    unnamed x4, other arithmetic: 26.2 us -> 0.01 us
    dot_general x10, matrix products: 122 us -> 146 us  [the longest x5 78.3 us: layer(): gate = jnp.dot(a, w[0], preferred_element_type=jnp.float32)]
    reduce_sum x1 -> x0, blocking collectives: 14.9 us -> none  [of_a_group(): jnp.sum(g * g)]
    reshape x3 -> x0, other arithmetic: 12.3 us -> none  [step(): t.reshape(-1, *t.shape[2:])]
    unnamed x49 -> x59, local copies, waits for them, and re-layouts: 30.1 us -> 23.6 us
  transfers between devices with their start and end apart: 9 -> 0, of which waited for: 7 -> 0; matrix products, arithmetic and copies ran while one was open for 21% -> 0% of each run, Pallas kernels for 0% -> 0%
where the time goes in v1:
time: 523 us; the launch traced here: 515 us
  Pallas kernels  283 us (54%)
  matrix products  203 us (39%)
  local copies, waits for them, and re-layouts  23.6 us (5%)
    pallas_call x1, Pallas kernels, exchange_and_update(): pl.pallas_call(functools.partial(comm_kernel, count), out_shape=[jax.Shap...  283 us
    dot_general x5, matrix products, layer(): gate = jnp.dot(a, w[0], preferred_element_type=jnp.float32)  78.3 us
    dot_general x5, matrix products, layer(): up = jnp.dot(a, w[1], preferred_element_type=jnp.float32)  67.7 us
    dot_general x5, matrix products, matmul(): jnp.dot(a, w, preferred_element_type=jnp.float32).astype(jnp.bfloat16)  56.5 us
    unnamed x59, local copies, waits for them, and re-layouts  23.6 us

profile of v1, /device:TPU:0, one launch (start us, length us, event | category | flops | bytes accessed | tf_op | source)
XLA Modules:
  0.0 515.4 jit_solution(17222224653145951513)
XLA Ops:
  0.6 3.0 copy.20
  4.2 12.8 %fusion.45 = f32[2048,2048]{1,0:T(8,128)} fusion(bf16[2,640,2048]{2,1,0:T(8,128)(2,1)} %refs_6_.1, bf16[1,2048,640]{2,1,0:T(8,128)(2,1)} %param.11, f32[2048]{0:T(1024)S(1)} %add_rsqrt_fusion), kind=kOutput, calls=%fused_computation.65 | convolution fusion | flops 5372641280 | bytes 22028288 | tf_op jit(solution)/shard_map/jvp()/dot_general | solution.py:324
  17.1 16.7 %multiply_convert_fusion.1 = (bf16[2048,2048]{1,0:T(8,128)(2,1)}, f32[2048,2048]{1,0:T(8,128)}) fusion(f32[2048,2048]{1,0:T(8,128)} %fusion.45, bf16[2,640,2048]{2,1,0:T(8,128)(2,1)} %refs_7_.1, bf16[1,2048,640]{2,1,0:T(8,128)(2,1)} %param.11, f32[2048]{0:T(1024)S(1)} %add_rsqrt_fusion), kind=kOutput, calls=%fused_computation.17 | convolution fusion | flops 5397807104 | bytes 47194112 | tf_op jit(solution)/shard_map/jvp()/dot_general | solution.py:325
  33.8 9.2 %fusion.19 = (f32[2048]{0:T(1024)S(1)}, bf16[2048,640]{0,1:T(8,128)(2,1)S(1)}) fusion(bf16[2048,2048]{1,0:T(8,128)(2,1)} %get-tuple-element.27, bf16[2,2048,640]{2,1,0:T(8,128)(2,1)} %refs_8_.1, bf16[1,2048,640]{1,2,0:T(8,128)(2,1)S(1)} %copy.20), kind=kOutput, calls=%fused_computation.37 | convolution fusion | flops 5375260672 | bytes 16261120 | tf_op jit(solution)/shard_map/jvp()/dot_general | solution.py:313
  43.0 13.3 %fusion.36 = f32[2048,2048]{1,0:T(8,128)} fusion(bf16[2,640,2048]{2,1,0:T(8,128)(2,1)} %refs_7_.1, bf16[2048,640]{0,1:T(8,128)(2,1)S(1)} %get-tuple-element.30, f32[2048]{0:T(1024)S(1)} %fusion.69), kind=kOutput, calls=%fused_computation.56 | convolution fusion | flops 5372641280 | bytes 22028288 | tf_op jit(solution)/shard_map/jvp()/dot_general | solution.py:325
  56.3 10.7 %convolution_convert_fusion.1 = bf16[2048,2048]{1,0:T(8,128)(2,1)} fusion(bf16[1,2048,640]{2,1,0:T(8,128)(2,1)S(1)} %copy-done.5, bf16[2,2048,640]{2,1,0:T(8,128)(2,1)} %refs_8_.1), kind=kOutput, calls=%fused_computation.29 | convolution fusion | flops 5372903424 | bytes 13631488 | tf_op jit(solution)/shard_map/transpose(jvp())/dot_general | solution.py:313
  67.0 24.9 %fusion.2 = (bf16[2048,2048]{1,0:T(8,128)(2,1)}, f32[2048,2048]{1,0:T(8,128)}) fusion(f32[2048,2048]{1,0:T(8,128)} %fusion.36, bf16[2048,2048]{1,0:T(8,128)(2,1)} %convolution_convert_fusion.1, bf16[2,640,2048]{2,1,0:T(8,128)(2,1)} %refs_6_.1, bf16[2048,640]{0,1:T(8,128)(2,1)} %copy-done.3, f32[2048]{0:T(1024)S(1)} %fusion.69), kind=kOutput, calls=%fused_computation.8 | convolution fusion | flops 5422972928 | bytes 55582720 | tf_op jit(solution)/shard_map/jvp()/dot_general | solution.py:324
  91.8 16.9 %fusion.22 = bf16[2048,640]{1,0:T(8,128)(2,1)} fusion(f32[2048,2048]{1,0:T(8,128)} %fusion.36, bf16[1,2048,640]{2,1,0:T(8,128)(2,1)} %param.12, f32[2048,2048]{1,0:T(8,128)} %get-tuple-element.32), kind=kOutput, calls=%fused_computation.41 | convolution fusion | flops 5395185664 | bytes 38797312 | tf_op jit(solution)/shard_map/transpose(jvp())/dot_general | solution.py:313
  108.7 10.4 %convolution_convert_fusion.4 = bf16[640,2048]{1,0:T(8,128)(2,1)} fusion(bf16[2048,2048]{1,0:T(8,128)(2,1)} %get-tuple-element.31, bf16[2048,640]{0,1:T(8,128)(2,1)S(1)} %copy-done.4, f32[2048]{0:T(1024)S(1)} %fusion.69), kind=kOutput, calls=%fused_computation.48 | convolution fusion | flops 5372641280 | bytes 13639680 | tf_op jit(solution)/shard_map/transpose(jvp())/dot_general | solution.py:324
  119.1 12.6 %fusion.23 = bf16[640,2048]{1,0:T(8,128)(2,1)} fusion(bf16[2048,2048]{1,0:T(8,128)(2,1)} %convolution_convert_fusion.1, bf16[2048,640]{0,1:T(8,128)(2,1)S(1)} %copy-done.4, f32[2048]{0:T(1024)S(1)} %fusion.69, f32[2048,2048]{1,0:T(8,128)} %get-tuple-element.32), kind=kOutput, calls=%fused_computation.42 | convolution fusion | flops 5399117824 | bytes 30416896 | tf_op jit(solution)/shard_map/transpose(jvp())/dot_general | solution.py:325
  131.7 12.6 %fusion.24 = bf16[2048,640]{0,1:T(8,128)(2,1)} fusion(bf16[2048,2048]{1,0:T(8,128)(2,1)} %convolution_convert_fusion.1, bf16[2,640,2048]{2,1,0:T(8,128)(2,1)S(1)} %bitcast.72, f32[2048,2048]{1,0:T(8,128)} %get-tuple-element.32), kind=kOutput, calls=%fused_computation.43 | convolution fusion | flops 5395185664 | bytes 30408704 | tf_op jit(solution)/shard_map/transpose(jvp())/dot_general | solution.py:325
  144.3 11.1 %fusion.21 = (f32[2048]{0:T(1024)S(1)}, bf16[2048,640]{0,1:T(8,128)(2,1)}) fusion(bf16[2048,640]{0,1:T(8,128)(2,1)S(1)} %copy-done.4, bf16[2048,640]{0,1:T(8,128)(2,1)} %fusion.24, bf16[2048,2048]{1,0:T(8,128)(2,1)} %get-tuple-element.31, bf16[2,640,2048]{2,1,0:T(8,128)(2,1)S(1)} %bitcast.74), kind=kOutput, calls=%fused_computation.39 | convolution fusion | flops 5375260672 | bytes 18882560 | tf_op jit(solution)/shard_map/transpose(jvp())/dot_general | solution.py:324
  155.5 3.0 copy.21
  158.5 4.4 fusion.31
  162.9 10.5 %convolution_convert_fusion.2 = bf16[2048,640]{1,0:T(8,128)(2,1)} fusion(bf16[2048,2048]{1,0:T(8,128)(2,1)} %get-tuple-element.27, bf16[2048,640]{0,1:T(8,128)(2,1)S(1)} %fusion.31), kind=kOutput, calls=%fused_computation.46 | convolution fusion | flops 5370019840 | bytes 13631488 | tf_op jit(solution)/shard_map/transpose(jvp())/dot_general | solution.py:313
  173.4 9.3 %convolution_convert_fusion = bf16[2048,2048]{1,0:T(8,128)(2,1)} fusion(bf16[2048,640]{0,1:T(8,128)(2,1)S(1)} %fusion.31, bf16[2,2048,640]{2,1,0:T(8,128)(2,1)S(1)} %bitcast.76), kind=kOutput, calls=%fused_computation.28 | convolution fusion | flops 5372903424 | bytes 13631488 | tf_op jit(solution)/shard_map/transpose(jvp())/dot_general | solution.py:313
  182.7 19.1 %fusion.25 = bf16[640,2048]{1,0:T(8,128)(2,1)} fusion(f32[2048,2048]{1,0:T(8,128)} %fusion.45, f32[2048,2048]{1,0:T(8,128)} %get-tuple-element.28, bf16[2048,2048]{1,0:T(8,128)(2,1)} %convolution_convert_fusion, bf16[1,2048,640]{1,2,0:T(8,128)(2,1)S(1)} %copy-done.1, f32[2048]{0:T(1024)S(1)} %copy-done.15), kind=kOutput, calls=%fused_computation.44 | convolution fusion | flops 5420089344 | bytes 47194112 | tf_op jit(solution)/shard_map/transpose(jvp())/dot_general | solution.py:324
  201.9 12.5 %fusion.28 = bf16[640,2048]{1,0:T(8,128)(2,1)} fusion(bf16[2048,2048]{1,0:T(8,128)(2,1)} %convolution_convert_fusion, f32[2048,2048]{1,0:T(8,128)} %fusion.45, bf16[1,2048,640]{1,2,0:T(8,128)(2,1)S(1)} %copy-done.1, f32[2048]{0:T(1024)S(1)} %copy-done.15), kind=kOutput, calls=%fused_computation.45 | convolution fusion | flops 5399117824 | bytes 30416896 | tf_op jit(solution)/shard_map/transpose(jvp())/dot_general | solution.py:325
  214.4 283.0 %reduce_step_gather.1 = (bf16[2,4,2,80,2048]{4,3,2,1,0:T(8,128)(2,1)}, bf16[2,4,2,80,2048]{4,3,2,1,0:T(8,128)(2,1)}, bf16[2,4,2,256,640]{4,3,2,1,0:T(8,128)(2,1)...) custom-call(bf16[4,2,256,640]{3,2,1,0:T(8,128)(2,1)} %bitcast.82, ...), custom_call_target="tpu_custom_call" | custom-call | tf_op jit(solution)/shard_map/reduce_step_gather/pallas_call | solution.py:282
  497.4 6.2 %copy.31 = bf16[2,640,2048]{2,1,0:T(8,128)(2,1)} copy(bf16[2,640,2048]{2,1,0:T(8,128)(2,1)} %bitcast.81) | data formatting | bytes 10485760
  503.6 2.4 copy.32
  505.9 2.7 copy.33
  508.6 1.1 copy.34
  509.7 1.1 copy.35
  (60 shorter events, 4.9 us)
Async XLA Ops:
  3.6 30.2 %copy-start = (bf16[1,2048,640]{1,2,0:T(8,128)(2,1)}, bf16[1,2048,640]{1,2,0:T(8,128)(2,1)S(1)}, u32[]{:S(2)}) copy-start(bf16[1,2048,640]{1,2,0:T(8,128)(2,1)S(1)} %copy.20) | copy-start | bytes 7864324
  4.2 12.8 %copy-start.14 = (f32[2048]{0:T(1024)}, f32[2048]{0:T(1024)S(1)}, u32[]{:S(2)}) copy-start(f32[2048]{0:T(1024)S(1)} %add_rsqrt_fusion) | copy-start | bytes 24580
  43.0 13.3 %copy-start.3 = (bf16[2048,640]{0,1:T(8,128)(2,1)}, bf16[2048,640]{0,1:T(8,128)(2,1)S(1)}, u32[]{:S(2)}) copy-start(bf16[2048,640]{0,1:T(8,128)(2,1)S(1)} %get-tuple-element.30) | copy-start | bytes 7864324
  43.0 13.3 %copy-start.12 = (f32[2048]{0:T(1024)}, f32[2048]{0:T(1024)S(1)}, u32[]{:S(2)}) copy-start(f32[2048]{0:T(1024)S(1)} %get-tuple-element.29) | copy-start | bytes 24580
  43.0 13.3 %copy-start.5 = (bf16[1,2048,640]{2,1,0:T(8,128)(2,1)S(1)}, bf16[1,2048,640]{2,1,0:T(8,128)(2,1)}, u32[]{:S(2)}) copy-start(bf16[1,2048,640]{2,1,0:T(8,128)(2,1)} %param.12) | copy-start | bytes 7864324
  91.8 16.9 %copy-start.4 = (bf16[2048,640]{0,1:T(8,128)(2,1)S(1)}, bf16[2048,640]{0,1:T(8,128)(2,1)}, u32[]{:S(2)}) copy-start(bf16[2048,640]{0,1:T(8,128)(2,1)} %copy-done.3) | copy-start | bytes 7864324
  108.7 23.0 %slice-start = ((s8[5242880]{0:T(1024)(128)(4,1)}), s8[4194304]{0:T(1024)(128)(4,1)S(1)}, s32[]{:S(2)}) async-start(s8[5242880]{0:T(1024)(128)(4,1)} %bitcast.71), calls=%async_computation | async-start | bytes 8388608
  119.1 12.6 %slice-start.1 = ((s8[5242880]{0:T(1024)(128)(4,1)}), s8[1048576]{0:T(1024)(128)(4,1)S(1)}, s32[]{:S(2)}) async-start(s8[5242880]{0:T(1024)(128)(4,1)} %bitcast.71), calls=%async_computation.1 | async-start | bytes 2097152
  119.1 25.2 %slice-start.2 = ((s8[5242880]{0:T(1024)(128)(4,1)}), s8[4194304]{0:T(1024)(128)(4,1)S(1)}, s32[]{:S(2)}) async-start(s8[5242880]{0:T(1024)(128)(4,1)} %bitcast.73), calls=%async_computation.2 | async-start | bytes 8388608
  131.7 12.6 %slice-start.3 = ((s8[5242880]{0:T(1024)(128)(4,1)}), s8[1048576]{0:T(1024)(128)(4,1)S(1)}, s32[]{:S(2)}) async-start(s8[5242880]{0:T(1024)(128)(4,1)} %bitcast.73), calls=%async_computation.3 | async-start | bytes 2097152
  155.5 3.0 copy-start.13
  158.5 14.9 %slice-start.4 = ((s8[5242880]{0:T(1024)(128)(4,1)}), s8[1048576]{0:T(1024)(128)(4,1)S(1)}, s32[]{:S(2)}) async-start(s8[5242880]{0:T(1024)(128)(4,1)} %bitcast.75), calls=%async_computation.4 | async-start | bytes 2097152
  162.9 10.5 %slice-start.5 = ((s8[5242880]{0:T(1024)(128)(4,1)}), s8[4194304]{0:T(1024)(128)(4,1)S(1)}, s32[]{:S(2)}) async-start(s8[5242880]{0:T(1024)(128)(4,1)} %bitcast.75), calls=%async_computation.5 | async-start | bytes 8388608
  173.4 9.3 %copy-start.1 = (bf16[1,2048,640]{1,2,0:T(8,128)(2,1)S(1)}, bf16[1,2048,640]{1,2,0:T(8,128)(2,1)}, u32[]{:S(2)}) copy-start(bf16[1,2048,640]{1,2,0:T(8,128)(2,1)} %copy-done) | copy-start | bytes 7864324
  173.4 9.3 %copy-start.15 = (f32[2048]{0:T(1024)S(1)}, f32[2048]{0:T(1024)}, u32[]{:S(2)}) copy-start(f32[2048]{0:T(1024)} %copy-done.14) | copy-start | bytes 24580
  497.4 6.2 %copy-start.2 = (bf16[2,4,2,80,2048]{4,3,2,1,0:T(8,128)(2,1)S(1)}, bf16[2,4,2,80,2048]{4,3,2,1,0:T(8,128)(2,1)}, u32[]{:S(2)}) copy-start(bf16[2,4,2,80,2048]{4,3,2,1,0:T(8,128)(2,1)} %get-tuple-element.19) | copy-start | bytes 15728644
  497.4 8.5 %slice-start.6 = ((s8[5242880]{0:T(1024)(128)(4,1)}), s8[4194304]{0:T(1024)(128)(4,1)S(1)}, s32[]{:S(2)}) async-start(s8[5242880]{0:T(1024)(128)(4,1)} %bitcast.77), calls=%async_computation.6 | async-start | bytes 8388608
  503.6 2.4 slice-start.7
  505.9 2.7 copy-start.11
  505.9 3.8 copy-start.10
  505.9 4.8 copy-start.9
  508.6 3.2 copy-start.8
  508.6 4.2 copy-start.7
  509.7 4.2 copy-start.6

commit v2 on v1

v2 whole, which is shorter than its diff:
```python
import functools

import jax
import jax.numpy as jnp
from jax import lax
from jax.experimental import pallas as pl
from jax.experimental.pallas import tpu as pltpu
from jax.sharding import PartitionSpec as P

NAMES = ("w_gate", "w_up", "w_down")
MESH = pl.DeviceIdType.MESH
F32, BF16 = jnp.float32, jnp.bfloat16
ORDER = ((1, 2), (1, 0), (1, 1), (0, 2), (0, 0), (0, 1))
N = len(ORDER)


def chunks(rows, body):
    @pl.loop(0, rows // 16)
    def _(t):
        body(pl.ds(pl.multiple_of(t * 16, 16), 16))


TOKENS, D, FF = 2048, 640, 2048
T, CH = 256, 512
PARTS = FF // CH
STATIC_UNROLL = 2


def nt(a, b):
    return lax.dot_general(a, b, (((1,), (1,)), ((), ())), preferred_element_type=F32)


def nn(a, b):
    return jnp.dot(a, b, preferred_element_type=F32)


def tile(t, size=T):
    return pl.ds(pl.multiple_of(t * size, size), size)


def scale_of(wide):
    return lax.rsqrt(jnp.mean(wide * wide, -1, keepdims=True) + 1e-6)


def compute(x_hbm, dy_hbm, w_hbm, full, h, a, a_t, d, d_t, acc, hid, dgate, dup, wg, wu, wd, in_sem, w_sem, after_tile, after_part):
    def weights(number):
        layer = jnp.where(number // PARTS == 1, 1, 0)
        at, slot = tile(lax.rem(number, PARTS), CH), lax.rem(number, 2)
        return (
            pltpu.make_async_copy(w_hbm[0].at[layer, :, at], wg.at[slot], w_sem.at[slot, 0]),
            pltpu.make_async_copy(w_hbm[1].at[layer, :, at], wu.at[slot], w_sem.at[slot, 1]),
            pltpu.make_async_copy(w_hbm[2].at[layer, at, :], wd.at[slot], w_sem.at[slot, 2]),
        )

    def next_weights(number):
        for copy in weights(number):
            copy.wait()

        @pl.when(number + 1 < 3 * PARTS)
        def _():
            for copy in weights(number + 1):
                copy.start()

        return lax.rem(number, 2)

    def norm_tile(at, wide):
        value = (wide * scale_of(wide)).astype(BF16)
        a[at, :] = value
        a_t[:, at] = value.T

    load_x = pltpu.make_async_copy(x_hbm, h, in_sem.at[0])
    load_dy = pltpu.make_async_copy(dy_hbm, d, in_sem.at[1])
    load_x.start()
    load_dy.start()
    for copy in weights(0):
        copy.start()
    load_x.wait()

    @pl.loop(0, TOKENS // T)
    def _(t):
        wide = h[tile(t), :].astype(F32)
        a[tile(t), :] = (wide * scale_of(wide)).astype(BF16)

    @pl.loop(0, PARTS)
    def _(c):
        slot = next_weights(c)

        def forward(t, first):
            at = tile(t)
            gate, up = nn(a[at, :], wg[slot]), nn(a[at, :], wu[slot])
            value = nn((gate * jax.nn.sigmoid(gate) * up).astype(BF16), wd[slot])
            if first:
                acc[at, :] = value
            else:
                acc[at, :] += value

        @pl.when(c == 0)
        def _():
            @pl.loop(0, TOKENS // T, unroll=STATIC_UNROLL)
            def _(t):
                forward(t, True)

        @pl.when(c > 0)
        def _():
            @pl.loop(0, TOKENS // T, unroll=STATIC_UNROLL)
            def _(t):
                forward(t, False)

    load_dy.wait()

    @pl.loop(0, TOKENS // T)
    def _(t):
        at = tile(t)
        value = h[at, :].astype(F32) + acc[at, :].astype(BF16).astype(F32)
        value = value.astype(BF16)
        h[at, :] = value
        norm_tile(at, value.astype(F32))
        d_t[:, at] = d[at, :].T
        acc[at, :] = jnp.zeros((T, D), F32)

    def backward(layer):
        @pl.loop(0, PARTS)
        def _(c):
            number = (2 - layer) * PARTS + c
            slot = next_weights(number)

            @pl.loop(0, TOKENS // T // STATIC_UNROLL)
            def _(pair):
                for half in range(STATIC_UNROLL):
                    at = tile(pair * STATIC_UNROLL + half)
                    gate, up = nn(a[at, :], wg[slot]), nn(a[at, :], wu[slot])
                    back = nt(d[at, :], wd[slot]).astype(BF16).astype(F32)
                    sig = jax.nn.sigmoid(gate)
                    silu = gate * sig
                    hid[at, :] = (silu * up).astype(BF16)
                    by_up = (back * silu).astype(BF16)
                    by_gate = (back * up * (sig + silu * (1.0 - sig))).astype(BF16)
                    dup[at, :] = by_up
                    dgate[at, :] = by_gate
                    if layer == 1:
                        acc[at, :] += nt(by_gate, wg[slot]) + nt(by_up, wu[slot])
                after_tile(number - PARTS, pair)

            @pl.loop(0, CH // 256)
            def _(n):
                here = tile(n, 256)
                there = pl.ds(pl.multiple_of(c * CH + n * 256, 256), 256)
                full[2][layer, c, n] = nn(d_t[...], hid[:, here]).astype(BF16).T
                full[0][layer, :, :, :, there] = nn(a_t[...], dgate[:, here]).astype(BF16).reshape(4, 2, D // 8, 256)
                full[1][layer, :, :, :, there] = nn(a_t[...], dup[:, here]).astype(BF16).reshape(4, 2, D // 8, 256)

            after_part(number - PARTS)

    backward(1)

    @pl.loop(0, TOKENS // T)
    def _(t):
        at = tile(t)
        wide = h[at, :].astype(F32)
        scale = scale_of(wide)
        by_a = acc[at, :].astype(BF16).astype(F32)
        by_h = scale * by_a - wide * (scale * scale * scale * jnp.mean(by_a * wide, -1, keepdims=True))
        value = (d[at, :].astype(F32) + by_h.astype(BF16).astype(F32)).astype(BF16)
        d[at, :] = value
        d_t[:, at] = value.T

    load_x.start()
    load_x.wait()

    @pl.loop(0, TOKENS // T)
    def _(t):
        norm_tile(tile(t), h[tile(t), :].astype(F32))

    backward(0)


COMPUTE_SCRATCH = [
    pltpu.VMEM((TOKENS, D), BF16),
    pltpu.VMEM((TOKENS, D), BF16),
    pltpu.VMEM((D, TOKENS), BF16),
    pltpu.VMEM((TOKENS, D), BF16),
    pltpu.VMEM((D, TOKENS), BF16),
    pltpu.VMEM((TOKENS, D), F32),
    pltpu.VMEM((TOKENS, CH), BF16),
    pltpu.VMEM((TOKENS, CH), BF16),
    pltpu.VMEM((TOKENS, CH), BF16),
    pltpu.VMEM((2, D, CH), BF16),
    pltpu.VMEM((2, D, CH), BF16),
    pltpu.VMEM((2, CH, D), BF16),
    pltpu.SemaphoreType.DMA((2,)),
    pltpu.SemaphoreType.DMA((2, 3)),
]


LAG = 2
UNITS = 2 * PARTS


def step_kernel(count, x_hbm, dy_hbm, *refs):
    w_in, m_in, v_in, refs = refs[:3], refs[3:6], refs[6:9], refs[9:]
    full, m_out, v_out, refs = refs[:3], refs[3:6], refs[6:9], refs[9:]
    scratch, refs = refs[: len(COMPUTE_SCRATCH)], refs[len(COMPUTE_SCRATCH) :]
    xs, rs, refs = refs[:3], refs[3:6], refs[6:]
    moments, squares, norms, load_sem, store_sem, x_send, x_recv, r_send, r_recv, n_send, n_recv, g_send, g_recv = refs
    a, a_t, acc = scratch[1], scratch[2], scratch[5]

    rep, me = lax.axis_index("rep"), lax.axis_index("dp")
    z, k = me // 2, lax.rem(me, 2)
    flip = z >= 2
    inner = jnp.logical_or(z == 1, z == 2)
    outer = jnp.logical_not(inner)

    def blk(mirrored):
        return jnp.where(flip, 3 - mirrored, mirrored)

    own = jnp.where(inner, blk(1), blk(0))
    ahead = jnp.where(flip, z - 1, z + 1)
    back = jnp.where(outer, z, jnp.where(flip, z + 1, z - 1))

    def device(zz, kk):
        return (rep, 2 * zz + kk)

    def remote(src, dst, send, recv, to):
        return pltpu.make_async_remote_copy(
            src_ref=src, dst_ref=dst, send_sem=send, recv_sem=recv, device_id=to, device_id_type=MESH
        )


    def place(u):
        c = lax.rem(u, PARTS)
        return 1 - u // PARTS, c, tile(c, CH)

    def exchange(u):
        layer, c, at = place(u)
        to = device(z, 1 - k)
        return [
            remote(full[m].at[layer, :, 1 - k, :, at], xs[m].at[layer, :, :, at], x_send.at[u, m], x_recv.at[u, m], to)
            for m in range(2)
        ] + [remote(full[2].at[layer, c, 1 - k], xs[2].at[layer, c], x_send.at[u, 2], x_recv.at[u, 2], to)]

    def hop(u, m, block, slot, send, to):
        layer, c, at = place(u)
        sems = r_send.at[u, m, send], r_recv.at[u, m, slot], device(to, k)
        if m == 2:
            return remote(full[2].at[layer, c, k], rs[2].at[layer, slot], *sems)
        return remote(full[m].at[layer, block, k, :, at], rs[m].at[layer, slot, :, at], *sems)

    def each(u, block, body):
        body(0)
        body(1)

        @pl.when(lax.rem(u, PARTS) == block)
        def _():
            body(2)

    def add(u, m, block, slots, square=False):
        layer, c, at = place(u)

        def part(rows, columns):
            x = xs[m][layer, block, rows, columns]
            total = full[m][layer, block, k, rows, columns].astype(F32) + x.astype(F32)
            for slot in slots:
                total += rs[m][layer, slot, rows, columns].astype(F32)
            total = total.astype(BF16)
            full[m][layer, block, k, rows, columns] = total
            if square:
                total = total.astype(F32)
                total = total * total
                folded = total[:8]
                for r in range(1, total.shape[0] // 8):
                    folded += total[r * 8 : (r + 1) * 8]
                sums = squares[...]
                for q in range(total.shape[1] // 128):
                    sums += folded[:, q * 128 : (q + 1) * 128]
                squares[...] = sums

        if m < 2:
            part(pl.ds(0, D // 8), at)
        else:

            @pl.loop(0, 4)
            def _(q):
                part(tile(q, FF // 32), pl.ds(0, D))

    def send_out(u):
        for copy in exchange(u):
            copy.wait_recv()

        @pl.when(outer)
        def _():
            for j in range(3):

                def body(m):
                    add(u, m, blk(3 - j), ())
                    hop(u, m, blk(3 - j), j, j, ahead).start()

                each(u, blk(3 - j), body)

    def pass_sum(u, j):
        block, come, go, to = ((3, 0, 3, ahead), (2, 1, 4, ahead), (0, 3, 0, back))[j]

        @pl.when(inner)
        def _():
            def body(m):
                hop(u, m, blk(block), come, j, ahead).wait_recv()
                add(u, m, blk(block), (come,))
                hop(u, m, blk(block), go, j, to).start()

            each(u, blk(block), body)

    def finish(u):
        @pl.when(outer)
        def _():
            def body(m):
                hop(u, m, own, 0, 0, ahead).wait_recv()
                add(u, m, own, (0,), True)

            each(u, own, body)

        @pl.when(inner)
        def _():
            def body(m):
                hop(u, m, own, 2, 2, ahead).wait_recv()
                hop(u, m, own, 4, 2, ahead).wait_recv()
                add(u, m, own, (2, 4), True)

            each(u, own, body)

    def sent(u):
        for copy in exchange(u):
            copy.wait_send()

        @pl.when(outer)
        def _():
            for j in range(3):
                each(u, blk(3 - j), lambda m: hop(u, m, blk(3 - j), j, j, ahead).wait_send())

        @pl.when(inner)
        def _():
            for j, block in enumerate((3, 2, 0)):
                each(u, blk(block), lambda m: hop(u, m, blk(block), 0, j, ahead).wait_send())

    def after_part(u):
        for copy in exchange(u):
            copy.start()

    def beside(u, p):
        @pl.when(jnp.logical_and(p == 0, u >= 1))
        def _():
            send_out(u - 1)

        @pl.when(jnp.logical_and(p == 1, u >= LAG))
        def _():
            pass_sum(u - LAG, 0)

        @pl.when(jnp.logical_and(p == 2, u >= LAG))
        def _():
            pass_sum(u - LAG, 1)

        @pl.when(jnp.logical_and(p == 2, u >= LAG + 1))
        def _():
            finish(u - LAG - 1)

        @pl.when(jnp.logical_and(p == 3, u >= LAG))
        def _():
            pass_sum(u - LAG, 2)

    squares[...] = jnp.zeros_like(squares)
    barrier = pltpu.get_barrier_semaphore()
    for p in range(1, 8):
        pl.semaphore_signal(barrier, inc=1, device_id=(rep, lax.rem(me + p, 8)), device_id_type=MESH)
    pl.semaphore_wait(barrier, 7)

    compute(x_hbm, dy_hbm, w_in, full, *scratch, beside, after_part)


    def holds(i):
        layer, which = ORDER[i]
        if which == 2:
            first = 512 * layer
            return acc.at[first : first + 256], acc.at[first + 256 : first + 512], a.at[256 * layer : 256 * layer + 256]
        old = (2 * layer + which) * (D // 8)
        return moments.at[which, 0], moments.at[which, 1], a_t.at[old : old + D // 8]

    def load(i):
        layer, which = ORDER[i]
        rows = m_in[which].shape[1]
        m, v, old = holds(i)
        return (
            pltpu.make_async_copy(m_in[which].at[layer], m, load_sem.at[i, 0]),
            pltpu.make_async_copy(v_in[which].at[layer], v, load_sem.at[i, 1]),
            pltpu.make_async_copy(w_in[which].at[layer, pl.ds(pl.multiple_of(me * rows, 16), rows)], old, load_sem.at[i, 2]),
        )

    def store(i):
        layer, which = ORDER[i]
        m, v, _ = holds(i)
        return (
            pltpu.make_async_copy(m, m_out[which].at[layer], store_sem.at[i, 0]),
            pltpu.make_async_copy(v, v_out[which].at[layer], store_sem.at[i, 1]),
        )

    for i in range(4):
        for copy in load(i):
            copy.start()

    send_out(UNITS - 1)
    for u in range(UNITS - LAG, UNITS):
        for j in range(3):
            pass_sum(u, j)
        finish(u - 1)
    finish(UNITS - 1)

    @pl.loop(0, UNITS)
    def _(u):
        sent(u)

    norms[me] = squares[...]

    def norm(p, src):
        return remote(norms.at[src], norms.at[src], n_send.at[p - 1], n_recv.at[src], (rep, lax.rem(me + p, 8)))

    for p in range(1, 8):
        norm(p, me).start()
    for p in range(1, 8):
        norm(p, lax.rem(me + p, 8)).wait_recv()
    total = norms[0]
    for other in range(1, 8):
        total += norms[other]
    ss = jnp.sum(total, keepdims=True)
    factor = jnp.minimum(1.0, 0.5 * lax.rsqrt(ss / count + 1e-30))

    def update(i):
        layer, which = ORDER[i]
        for copy in load(i):
            copy.wait()
        mine = full[which].at[layer, own, k]
        m, v, w = holds(i)

        def body(at):
            g = mine[at, :].astype(F32) * factor
            new_m = 0.9 * m[at, :] + 0.1 * g
            new_v = 0.95 * v[at, :] + 0.05 * g * g
            old = w[at, :].astype(F32)
            step = new_m * lax.rsqrt(new_v + 1e-8) + 0.1 * old
            m[at, :] = new_m
            v[at, :] = new_v
            mine[at, :] = (old - 0.02 * step).astype(BF16)

        chunks(mine.shape[0], body)
        for copy in store(i):
            copy.start()

    def pass_on(i, block, which_way, to, plane):
        layer, which = ORDER[i]
        here = full[which].at[layer, block, plane]
        return remote(here, here, g_send.at[i, block, which_way], g_recv.at[i, block, plane], to)

    def ahead_copy(i, block):
        return pass_on(i, block, 0, device(ahead, k), k)

    def back_copy(i, block):
        return pass_on(i, block, 1, device(back, k), k)

    def across_copy(i, block):
        return pass_on(i, block, 2, device(z, 1 - k), k)

    for s in range(N + 3):
        if s < N:
            if s >= 4:
                for copy in store(s - 3):
                    copy.wait()
                for copy in load(s):
                    copy.start()
            update(s)

            @pl.when(inner)
            def _():
                back_copy(s, own).start()

            ahead_copy(s, own).start()
            across_copy(s, own).start()
        if 0 <= s - 1 < N:
            i = s - 1

            @pl.when(outer)
            def _():
                ahead_copy(i, blk(1)).wait_recv()
                across_copy(i, blk(1)).start()

            @pl.when(inner)
            def _():
                ahead_copy(i, blk(2)).wait_recv()
                back_copy(i, blk(2)).start()
                across_copy(i, blk(2)).start()
                ahead_copy(i, blk(0)).wait_recv()
                ahead_copy(i, blk(0)).start()
                across_copy(i, blk(0)).start()

        if 0 <= s - 2 < N:
            i = s - 2

            @pl.when(outer)
            def _():
                ahead_copy(i, blk(2)).wait_recv()
                across_copy(i, blk(2)).start()

            @pl.when(inner)
            def _():
                ahead_copy(i, blk(3)).wait_recv()
                back_copy(i, blk(3)).start()
                across_copy(i, blk(3)).start()

        if 0 <= s - 3 < N:
            i = s - 3

            @pl.when(outer)
            def _():
                ahead_copy(i, blk(3)).wait_recv()
                across_copy(i, blk(3)).start()

    for p in range(1, 8):
        norm(p, me).wait_send()
    for i in range(N):
        if i in (0, 3, 4, 5):
            for copy in store(i):
                copy.wait()
        for b in range(4):
            pass_on(i, b, 2, device(z, 1 - k), 1 - k).wait_recv()
            across_copy(i, b).wait_send()
        ahead_copy(i, own).wait_send()

        @pl.when(inner)
        def _():
            ahead_copy(i, blk(0)).wait_send()
            for b in range(1, 4):
                back_copy(i, blk(b)).wait_send()


def solution(mesh):
    def step(x, dy, *arrays):
        weights = arrays[:3]
        dims = [(w.shape[0], w.shape[1] // 8, w.shape[2]) for w in weights]
        count = float(sum(w.size for w in weights))
        any_space = pl.BlockSpec(memory_space=pl.ANY)
        vmem = pl.BlockSpec(memory_space=pltpu.VMEM)
        dma = pltpu.SemaphoreType.DMA
        out = pl.pallas_call(
            functools.partial(step_kernel, count),
            out_shape=[jax.ShapeDtypeStruct((l, 4, 2, r, c), BF16) for l, r, c in dims]
            + [jax.ShapeDtypeStruct(d, F32) for d in dims] * 2,
            in_specs=[any_space] * 11,
            out_specs=[vmem] * 3 + [any_space] * 6,
            scratch_shapes=COMPUTE_SCRATCH
            + [pltpu.VMEM((l, 4, r, c), BF16) for l, r, c in dims]
            + [pltpu.VMEM((l, 5, r, c), BF16) for l, r, c in dims]
            + [
                pltpu.VMEM((2, 2, D // 8, FF), F32),
                pltpu.VMEM((8, 128), F32),
                pltpu.VMEM((8, 8, 128), F32),
                dma((N, 3)),
                dma((N, 2)),
                dma((UNITS, 3)),
                dma((UNITS, 3)),
                dma((UNITS, 3, 3)),
                dma((UNITS, 3, 5)),
                dma((7,)),
                dma((8,)),
                dma((N, 4, 3)),
                dma((N, 4, 2)),
            ],
            compiler_params=pltpu.CompilerParams(collective_id=0, has_side_effects=True, vmem_limit_bytes=67043328),
            name="training_step",
        )(x[0], dy[0], *arrays)
        return tuple(o.reshape(w.shape) for o, w in zip(out[:3], weights)) + tuple(out[3:])

    every, rows, whole = P(("rep", "dp")), P(None, "dp"), P(None)
    return jax.shard_map(
        step,
        mesh=mesh,
        in_specs=(every, every, whole, whole, whole) + (rows,) * 6,
        out_specs=(P("rep"),) * 3 + (P("rep", "dp"),) * 6,
        check_vma=False,
    )
```

time: 523 us -> 382 us (0.73); the launches traced: 515 us -> 381 us
  matrix products: 203 us -> 0 us
  Pallas kernels: 283 us -> 360 us
    dot_general x15 -> x0, matrix products: 203 us -> none  [the longest x5 78.3 us: layer(): gate = jnp.dot(a, w[0], preferred_element_type=jnp.float32)]
    pallas_call x1, Pallas kernels: 283 us -> 360 us  [step(): pl.pallas_call(functools.partial(step_kernel, count), out_shape=[jax.Shap...]
    unnamed x59 -> x27, local copies, waits for them, and re-layouts: 23.6 us -> 20.9 us
where the time goes in v2:
time: 382 us; the launch traced here: 381 us
  Pallas kernels  360 us (94%)
  local copies, waits for them, and re-layouts  20.9 us (5%)
    pallas_call x1, Pallas kernels, step(): pl.pallas_call(functools.partial(step_kernel, count), out_shape=[jax.Shap...  360 us
    unnamed x27, local copies, waits for them, and re-layouts  20.9 us

profile of v2, /device:TPU:0, one launch (start us, length us, event | category | flops | bytes accessed | tf_op | source)
XLA Modules:
  0.0 381.2 jit_solution(11435606647308541820)
XLA Ops:
  0.6 359.6 %training_step.1 = (bf16[2,4,2,80,2048]{4,3,2,1,0:T(8,128)(2,1)}, bf16[2,4,2,80,2048]{4,3,2,1,0:T(8,128)(2,1)}, bf16[2,4,2,256,640]{4,3,2,1,0:T(8,128)(2,1)}, f3...) custom-call(bf16[2048,640]{1,0:T(8,128)(2,1)} %bitcast.10, ...), custom_call_target="tpu_custom_call" | custom-call | tf_op jit(solution)/shard_map/training_step/pallas_call | solution.py:548
  360.3 0.0 copy-start
  360.3 0.0 slice-start
  360.3 6.2 %copy.29 = bf16[2,640,2048]{2,1,0:T(8,128)(2,1)} copy(bf16[2,640,2048]{2,1,0:T(8,128)(2,1)} %bitcast.9) | data formatting | bytes 10485760
  366.4 0.0 copy-done
  366.4 0.0 slice-start.1
  366.4 2.4 copy.30
  368.8 0.0 slice-done
  368.8 0.0 slice-done.1
  368.8 0.0 copy-start.6
  368.8 2.4 copy.31
  371.2 0.0 copy-done.6
  371.2 0.0 copy-start.5
  371.2 1.1 copy.32
  372.2 0.7 copy-done.5
  373.0 1.1 copy.33
  374.0 0.7 copy-done.4
  374.8 1.1 copy.34
  375.8 0.7 copy-done.3
  376.5 1.1 copy.35
  377.6 0.7 copy-done.2
  378.3 1.1 copy.36
  379.4 0.7 copy-done.1
  380.1 1.1 copy.37
  (5 shorter events, 0.0 us)
Async XLA Ops:
  360.3 6.2 %copy-start = (bf16[2,4,2,80,2048]{4,3,2,1,0:T(8,128)(2,1)S(1)}, bf16[2,4,2,80,2048]{4,3,2,1,0:T(8,128)(2,1)}, u32[]{:S(2)}) copy-start(bf16[2,4,2,80,2048]{4,3,2,1,0:T(8,128)(2,1)} %get-tuple-element.19) | copy-start | bytes 15728644
  360.3 8.5 %slice-start = ((s8[5242880]{0:T(1024)(128)(4,1)}), s8[4194304]{0:T(1024)(128)(4,1)S(1)}, s32[]{:S(2)}) async-start(s8[5242880]{0:T(1024)(128)(4,1)} %bitcast.5), calls=%async_computation | async-start | bytes 8388608
  366.4 2.4 slice-start.1
  368.8 2.4 copy-start.6
  371.2 1.8 copy-start.5
  373.0 1.8 copy-start.4
  374.8 1.8 copy-start.3
  376.5 1.8 copy-start.2
  378.3 1.8 copy-start.1

commit v3 on v2

--- a/solution.py
+++ b/solution.py
@@ -21,9 +21,9 @@
 
 
 TOKENS, D, FF = 2048, 640, 2048
-T, CH = 256, 512
+T, CH = 512, 512
 PARTS = FF // CH
-STATIC_UNROLL = 2
+STATIC_UNROLL = 1
 
 
 def nt(a, b):
@@ -194,14 +194,18 @@
 
 LAG = 2
 UNITS = 2 * PARTS
+QUARTERS, ROWS = 4, FF // 32
+PIECES = 2 + QUARTERS
 
 
 def step_kernel(count, x_hbm, dy_hbm, *refs):
     w_in, m_in, v_in, refs = refs[:3], refs[3:6], refs[6:9], refs[9:]
-    full, m_out, v_out, refs = refs[:3], refs[3:6], refs[6:9], refs[9:]
+    w_out, m_out, v_out, m_lent, v_lent, refs = refs[:3], refs[3:6], refs[6:9], refs[9:12], refs[12:15], refs[15:]
+    full, refs = refs[:3], refs[3:]
     scratch, refs = refs[: len(COMPUTE_SCRATCH)], refs[len(COMPUTE_SCRATCH) :]
     xs, rs, refs = refs[:3], refs[3:6], refs[6:]
-    moments, squares, norms, load_sem, store_sem, x_send, x_recv, r_send, r_recv, n_send, n_recv, g_send, g_recv = refs
+    moments, squares, norms, load_sem, store_sem, x_send, x_recv, r_send, r_recv, n_send, n_recv, g_send, g_recv, refs = *refs[:13], refs[13:]
+    lend_send, lend_recv, sum_send, sum_recv, keep_sem, extra_sem, give_send, give_recv = refs
     a, a_t, acc = scratch[1], scratch[2], scratch[5]
 
     rep, me = lax.axis_index("rep"), lax.axis_index("dp")
@@ -241,8 +245,9 @@
     def hop(u, m, block, slot, send, to):
         layer, c, at = place(u)
         sems = r_send.at[u, m, send], r_recv.at[u, m, slot], device(to, k)
-        if m == 2:
-            return remote(full[2].at[layer, c, k], rs[2].at[layer, slot], *sems)
+        if m >= 2:
+            rows = pl.ds((m - 2) * ROWS, ROWS)
+            return remote(full[2].at[layer, c, k, rows], rs[2].at[layer, slot, rows], *sems)
         return remote(full[m].at[layer, block, k, :, at], rs[m].at[layer, slot, :, at], *sems)
 
     def each(u, block, body):
@@ -251,18 +256,20 @@
 
         @pl.when(lax.rem(u, PARTS) == block)
         def _():
-            body(2)
+            for m in range(2, PIECES):
+                body(m)
 
     def add(u, m, block, slots, square=False):
         layer, c, at = place(u)
+        w = min(m, 2)
 
         def part(rows, columns):
-            x = xs[m][layer, block, rows, columns]
-            total = full[m][layer, block, k, rows, columns].astype(F32) + x.astype(F32)
+            x = xs[w][layer, block, rows, columns]
+            total = full[w][layer, block, k, rows, columns].astype(F32) + x.astype(F32)
             for slot in slots:
-                total += rs[m][layer, slot, rows, columns].astype(F32)
+                total += rs[w][layer, slot, rows, columns].astype(F32)
             total = total.astype(BF16)
-            full[m][layer, block, k, rows, columns] = total
+            full[w][layer, block, k, rows, columns] = total
             if square:
                 total = total.astype(F32)
                 total = total * total
@@ -277,10 +284,33 @@
         if m < 2:
             part(pl.ds(0, D // 8), at)
         else:
-
-            @pl.loop(0, 4)
-            def _(q):
-                part(tile(q, FF // 32), pl.ds(0, D))
+            part(pl.ds((m - 2) * ROWS, ROWS), pl.ds(0, D))
+
+
+    def when(condition, body):
+        if not isinstance(condition, bool):
+            pl.when(condition)(body)
+        elif condition:
+            body()
+
+    def lend(which):
+        to = device(back, k)
+        return (
+            remote(m_in[which].at[0], m_lent[which], lend_send.at[which, 0], lend_recv.at[which, 0], to),
+            remote(v_in[which].at[0], v_lent[which], lend_send.at[which, 1], lend_recv.at[which, 1], to),
+        )
+
+    def partial(u, m):
+        _, c, at = place(u)
+        sems = sum_send.at[c, m], sum_recv.at[c, m], device(back, k)
+        if m >= 2:
+            rows = pl.ds((m - 2) * ROWS, ROWS)
+            return remote(full[2].at[0, c, k, rows], rs[2].at[0, 1, rows], *sems)
+        return remote(full[m].at[0, own, k, :, at], rs[m].at[0, 1, :, at], *sems)
+
+    def give(which):
+        here = full[which].at[0, blk(1), k]
+        return remote(here, rs[which].at[0, 2], give_send.at[which], give_recv.at[which], device(ahead, k))
 
     def send_out(u):
         for copy in exchange(u):
@@ -294,7 +324,7 @@
                     add(u, m, blk(3 - j), ())
                     hop(u, m, blk(3 - j), j, j, ahead).start()
 
-                each(u, blk(3 - j), body)
+                when(j < 2 or u < PARTS, lambda: each(u, blk(3 - j), body))
 
     def pass_sum(u, j):
         block, come, go, to = ((3, 0, 3, ahead), (2, 1, 4, ahead), (0, 3, 0, back))[j]
@@ -317,12 +347,26 @@
 
             each(u, own, body)
 
+            def theirs(m):
+                partial(u, m).wait_recv()
+                add(u, m, blk(1), (1,), True)
+
+            when(u >= PARTS, lambda: each(u, blk(1), theirs))
+
+        def body(m):
+            hop(u, m, own, 2, 2, ahead).wait_recv()
+            hop(u, m, own, 4, 2, ahead).wait_recv()
+            add(u, m, own, (2, 4), True)
+
+        when(u < PARTS, lambda: pl.when(inner)(lambda: each(u, own, body)))
+
+    def pass_out(u):
         @pl.when(inner)
         def _():
             def body(m):
-                hop(u, m, own, 2, 2, ahead).wait_recv()
                 hop(u, m, own, 4, 2, ahead).wait_recv()
-                add(u, m, own, (2, 4), True)
+                add(u, m, own, (4,))
+                partial(u, m).start()
 
             each(u, own, body)
 
@@ -333,12 +377,16 @@
         @pl.when(outer)
         def _():
             for j in range(3):
-                each(u, blk(3 - j), lambda m: hop(u, m, blk(3 - j), j, j, ahead).wait_send())
+                when(
+                    j < 2 or u < PARTS,
+                    lambda: each(u, blk(3 - j), lambda m: hop(u, m, blk(3 - j), j, j, ahead).wait_send()),
+                )
 
         @pl.when(inner)
         def _():
             for j, block in enumerate((3, 2, 0)):
                 each(u, blk(block), lambda m: hop(u, m, blk(block), 0, j, ahead).wait_send())
+            when(u >= PARTS, lambda: each(u, own, lambda m: partial(u, m).wait_send()))
 
     def after_part(u):
         for copy in exchange(u):
@@ -357,19 +405,29 @@
         def _():
             pass_sum(u - LAG, 1)
 
-        @pl.when(jnp.logical_and(p == 2, u >= LAG + 1))
-        def _():
-            finish(u - LAG - 1)
-
-        @pl.when(jnp.logical_and(p == 3, u >= LAG))
-        def _():
-            pass_sum(u - LAG, 2)
+        @pl.when(jnp.logical_and(p == 2, u >= LAG + 2))
+        def _():
+            finish(u - LAG - 2)
+
+        @pl.when(jnp.logical_and(p == 3, u >= LAG + 1))
+        def _():
+            pass_sum(u - LAG - 1, 2)
+
+        @pl.when(jnp.logical_and(p == 3, u >= LAG + PARTS + 1))
+        def _():
+            pass_out(u - LAG - 1)
 
     squares[...] = jnp.zeros_like(squares)
     barrier = pltpu.get_barrier_semaphore()
     for p in range(1, 8):
         pl.semaphore_signal(barrier, inc=1, device_id=(rep, lax.rem(me + p, 8)), device_id_type=MESH)
     pl.semaphore_wait(barrier, 7)
+
+    @pl.when(inner)
+    def _():
+        for which in range(3):
+            for copy in lend(which):
+                copy.start()
 
     compute(x_hbm, dy_hbm, w_in, full, *scratch, beside, after_part)
 
@@ -380,7 +438,7 @@
             first = 512 * layer
             return acc.at[first : first + 256], acc.at[first + 256 : first + 512], a.at[256 * layer : 256 * layer + 256]
         old = (2 * layer + which) * (D // 8)
-        return moments.at[which, 0], moments.at[which, 1], a_t.at[old : old + D // 8]
+        return moments.at[0], moments.at[1], a_t.at[old : old + D // 8]
 
     def load(i):
         layer, which = ORDER[i]
@@ -400,16 +458,25 @@
             pltpu.make_async_copy(v, v_out[which].at[layer], store_sem.at[i, 1]),
         )
 
-    for i in range(4):
+    for i in (0, 1, 3):
         for copy in load(i):
             copy.start()
 
     send_out(UNITS - 1)
-    for u in range(UNITS - LAG, UNITS):
-        for j in range(3):
-            pass_sum(u, j)
-        finish(u - 1)
-    finish(UNITS - 1)
+    pass_sum(6, 0)
+    pass_sum(5, 2)
+    pass_out(5)
+    pass_sum(6, 1)
+    pass_sum(7, 0)
+    pass_sum(6, 2)
+    pass_out(6)
+    finish(4)
+    pass_sum(7, 1)
+    finish(5)
+    pass_sum(7, 2)
+    pass_out(7)
+    finish(6)
+    finish(7)
 
     @pl.loop(0, UNITS)
     def _(u):
@@ -430,63 +497,113 @@
     ss = jnp.sum(total, keepdims=True)
     factor = jnp.minimum(1.0, 0.5 * lax.rsqrt(ss / count + 1e-30))
 
-    def update(i):
-        layer, which = ORDER[i]
-        for copy in load(i):
-            copy.wait()
-        mine = full[which].at[layer, own, k]
-        m, v, w = holds(i)
-
+    def step_block(grad, m, v, w, new):
         def body(at):
-            g = mine[at, :].astype(F32) * factor
+            g = grad[at, :].astype(F32) * factor
             new_m = 0.9 * m[at, :] + 0.1 * g
             new_v = 0.95 * v[at, :] + 0.05 * g * g
             old = w[at, :].astype(F32)
             step = new_m * lax.rsqrt(new_v + 1e-8) + 0.1 * old
             m[at, :] = new_m
             v[at, :] = new_v
-            mine[at, :] = (old - 0.02 * step).astype(BF16)
-
-        chunks(mine.shape[0], body)
-        for copy in store(i):
+            new[at, :] = (old - 0.02 * step).astype(BF16)
+
+        chunks(new.shape[0], body)
+
+    def update(i):
+        layer, which = ORDER[i]
+        for copy in load(i):
+            copy.wait()
+        if layer == 1:
+            step_block(mine(i), *holds(i), mine(i))
+            return
+
+        @pl.when(outer)
+        def _():
+            step_block(mine(i), *holds(i), mine(i))
+
+        @pl.when(inner)
+        def _():
+            give(which).wait_recv()
+            step_block(rs[which].at[0, 2], *holds(i), mine(i))
+
+    def keep(i, block, src):
+        layer, which = ORDER[i]
+        return pltpu.make_async_copy(src, w_out[which].at[layer, block, k], keep_sem.at[i, jnp.where(block == own, 0, 1)])
+
+    def mine(i):
+        layer, which = ORDER[i]
+        return full[which].at[layer, own, k]
+
+    def extra(i):
+        _, which = ORDER[i]
+        rows = m_in[which].shape[1]
+        m, v = (acc.at[1024:1280], acc.at[1280:1536]) if which == 2 else (moments.at[0], moments.at[1])
+        new, old = rs[which].at[0, 2], rs[which].at[0, 3]
+        first = pl.multiple_of((2 * blk(1) + k) * rows, 16)
+        for copy in lend(which):
+            copy.wait_recv()
+        loads = (
+            pltpu.make_async_copy(m_lent[which], m, extra_sem.at[which, 0]),
+            pltpu.make_async_copy(v_lent[which], v, extra_sem.at[which, 1]),
+            pltpu.make_async_copy(w_in[which].at[0, pl.ds(first, rows)], old, extra_sem.at[which, 2]),
+        )
+        for copy in loads:
             copy.start()
-
-    def pass_on(i, block, which_way, to, plane):
+        for copy in loads:
+            copy.wait()
+        step_block(full[which].at[0, blk(1), k], m, v, old, new)
+        keep(i, blk(1), new).start()
+        across_copy(i, blk(1), new).start()
+
+    def pass_on(i, block, which_way, to, plane, src):
         layer, which = ORDER[i]
-        here = full[which].at[layer, block, plane]
-        return remote(here, here, g_send.at[i, block, which_way], g_recv.at[i, block, plane], to)
-
-    def ahead_copy(i, block):
-        return pass_on(i, block, 0, device(ahead, k), k)
-
-    def back_copy(i, block):
-        return pass_on(i, block, 1, device(back, k), k)
-
-    def across_copy(i, block):
-        return pass_on(i, block, 2, device(z, 1 - k), k)
+        here = w_out[which].at[layer, block, plane]
+        return remote(here if src is None else src, here, g_send.at[i, block, which_way], g_recv.at[i, block, plane], to)
+
+    def ahead_copy(i, block, src=None):
+        return pass_on(i, block, 0, device(ahead, k), k, src)
+
+    def back_copy(i, block, src=None):
+        return pass_on(i, block, 1, device(back, k), k, src)
+
+    def across_copy(i, block, src=None):
+        return pass_on(i, block, 2, device(z, 1 - k), k, src)
 
     for s in range(N + 3):
         if s < N:
-            if s >= 4:
-                for copy in store(s - 3):
+            before = {2: 1, 4: 2, 5: 4}.get(s)
+            if before is not None:
+                for copy in store(before):
                     copy.wait()
                 for copy in load(s):
                     copy.start()
             update(s)
-
-            @pl.when(inner)
-            def _():
-                back_copy(s, own).start()
-
-            ahead_copy(s, own).start()
-            across_copy(s, own).start()
+            if ORDER[s][0] == 1:
+
+                @pl.when(inner)
+                def _():
+                    back_copy(s, own, mine(s)).start()
+
+            ahead_copy(s, own, mine(s)).start()
+            across_copy(s, own, mine(s)).start()
+            if s in (1, 2, 3):
+
+                @pl.when(outer)
+                def _():
+                    give((2, 0, 1)[s - 1]).start()
+
+            keep(s, own, mine(s)).start()
+            for copy in store(s):
+                copy.start()
         if 0 <= s - 1 < N:
             i = s - 1
-
-            @pl.when(outer)
-            def _():
-                ahead_copy(i, blk(1)).wait_recv()
-                across_copy(i, blk(1)).start()
+            if ORDER[i][0] == 1:
+
+                @pl.when(outer)
+                def _():
+                    ahead_copy(i, blk(1)).wait_recv()
+                    across_copy(i, blk(1)).start()
 
             @pl.when(inner)
             def _():
@@ -497,6 +614,16 @@
                 ahead_copy(i, blk(0)).start()
                 across_copy(i, blk(0)).start()
 
+        if s >= N:
+            i = (3, 4, 5)[s - N]
+            if i == 4:
+                for copy in store(5):
+                    copy.wait()
+
+            @pl.when(outer)
+            def _():
+                extra(i)
+
         if 0 <= s - 2 < N:
             i = s - 2
 
@@ -522,19 +649,63 @@
     for p in range(1, 8):
         norm(p, me).wait_send()
     for i in range(N):
-        if i in (0, 3, 4, 5):
+        layer, which = ORDER[i]
+        if i in (0, 3):
             for copy in store(i):
                 copy.wait()
+        keep(i, own, mine(i)).wait()
         for b in range(4):
-            pass_on(i, b, 2, device(z, 1 - k), 1 - k).wait_recv()
+            pass_on(i, b, 2, device(z, 1 - k), 1 - k, None).wait_recv()
             across_copy(i, b).wait_send()
         ahead_copy(i, own).wait_send()
+        if layer == 0:
+
+            @pl.when(outer)
+            def _():
+                keep(i, blk(1), rs[which].at[0, 2]).wait()
+                give(which).wait_send()
 
         @pl.when(inner)
         def _():
             ahead_copy(i, blk(0)).wait_send()
-            for b in range(1, 4):
+            for b in range(1 if layer == 1 else 2, 4):
                 back_copy(i, blk(b)).wait_send()
+            if layer == 0:
+                for copy in lend(which):
+                    copy.wait_send()
+
+
+def copy_kernel(*refs):
+    ins, outs, held, (in_sem, out_sem) = refs[:9], refs[9:18], refs[18:27], refs[27:]
+
+    def each(sem, sources, targets):
+        return [
+            pltpu.make_async_copy(sources[n].at[layer], targets[n].at[layer], sem.at[n, layer])
+            for n in range(9)
+            for layer in range(2)
+        ]
+
+    loads, stores = each(in_sem, ins, held), each(out_sem, held, outs)
+    for load in loads:
+        load.start()
+    for load, store in zip(loads, stores):
+        load.wait()
+        store.start()
+    for store in stores:
+        store.wait()
+
+
+def copied(arrays):
+    any_space = pl.BlockSpec(memory_space=pl.ANY)
+    return pl.pallas_call(
+        copy_kernel,
+        out_shape=[jax.ShapeDtypeStruct(t.shape, t.dtype) for t in arrays],
+        in_specs=[any_space] * 9,
+        out_specs=[any_space] * 9,
+        scratch_shapes=[pltpu.VMEM(t.shape, t.dtype) for t in arrays] + [pltpu.SemaphoreType.DMA((9, 2))] * 2,
+        compiler_params=pltpu.CompilerParams(vmem_limit_bytes=67043328),
+        name="results",
+    )(*arrays)
 
 
 def solution(mesh):
@@ -543,36 +714,45 @@
         dims = [(w.shape[0], w.shape[1] // 8, w.shape[2]) for w in weights]
         count = float(sum(w.size for w in weights))
         any_space = pl.BlockSpec(memory_space=pl.ANY)
-        vmem = pl.BlockSpec(memory_space=pltpu.VMEM)
         dma = pltpu.SemaphoreType.DMA
         out = pl.pallas_call(
             functools.partial(step_kernel, count),
             out_shape=[jax.ShapeDtypeStruct((l, 4, 2, r, c), BF16) for l, r, c in dims]
-            + [jax.ShapeDtypeStruct(d, F32) for d in dims] * 2,
+            + [jax.ShapeDtypeStruct(d, F32) for d in dims] * 2
+            + [jax.ShapeDtypeStruct(d[1:], F32) for d in dims] * 2,
             in_specs=[any_space] * 11,
-            out_specs=[vmem] * 3 + [any_space] * 6,
-            scratch_shapes=COMPUTE_SCRATCH
+            out_specs=[any_space] * 15,
+            scratch_shapes=[pltpu.VMEM((l, 4, 2, r, c), BF16) for l, r, c in dims]
+            + COMPUTE_SCRATCH
             + [pltpu.VMEM((l, 4, r, c), BF16) for l, r, c in dims]
             + [pltpu.VMEM((l, 5, r, c), BF16) for l, r, c in dims]
             + [
-                pltpu.VMEM((2, 2, D // 8, FF), F32),
+                pltpu.VMEM((2, D // 8, FF), F32),
                 pltpu.VMEM((8, 128), F32),
                 pltpu.VMEM((8, 8, 128), F32),
                 dma((N, 3)),
                 dma((N, 2)),
                 dma((UNITS, 3)),
                 dma((UNITS, 3)),
-                dma((UNITS, 3, 3)),
-                dma((UNITS, 3, 5)),
+                dma((UNITS, PIECES, 3)),
+                dma((UNITS, PIECES, 5)),
                 dma((7,)),
                 dma((8,)),
                 dma((N, 4, 3)),
                 dma((N, 4, 2)),
+                dma((3, 2)),
+                dma((3, 2)),
+                dma((PARTS, PIECES)),
+                dma((PARTS, PIECES)),
+                dma((N, 2)),
+                dma((3, 3)),
+                dma((3,)),
+                dma((3,)),
             ],
             compiler_params=pltpu.CompilerParams(collective_id=0, has_side_effects=True, vmem_limit_bytes=67043328),
             name="training_step",
         )(x[0], dy[0], *arrays)
-        return tuple(o.reshape(w.shape) for o, w in zip(out[:3], weights)) + tuple(out[3:])
+        return tuple(copied([o.reshape(w.shape) for o, w in zip(out[:3], weights)] + list(out[3:9])))
 
     every, rows, whole = P(("rep", "dp")), P(None, "dp"), P(None)
     return jax.shard_map(

time: 382 us -> 325 us (0.85)
  Pallas kernels: 360 us -> 324 us
  local copies, waits for them, and re-layouts: 20.9 us -> 0 us
    pallas_call x1, Pallas kernels: 360 us -> 308 us  [step(): pl.pallas_call(functools.partial(step_kernel, count), out_shape=[jax.Shap...]
    unnamed x27 -> x0, local copies, waits for them, and re-layouts: 20.9 us -> none
    pallas_call x0 -> x1, Pallas kernels: none -> 16.6 us  [copied(): pl.pallas_call(copy_kernel, out_shape=[jax.ShapeDtypeStruct(t.shape, t.dt...]
where the time goes in v3:
time: 325 us
  Pallas kernels  324 us (100%)
    pallas_call x1, Pallas kernels, step(): pl.pallas_call(functools.partial(step_kernel, count), out_shape=[jax.Shap...  308 us
    pallas_call x1, Pallas kernels, copied(): pl.pallas_call(copy_kernel, out_shape=[jax.ShapeDtypeStruct(t.shape, t.dt...  16.6 us

profile of v3, /device:TPU:0, one launch (start us, length us, event | category | flops | bytes accessed | tf_op | source)
XLA Modules:
  0.0 325.0 jit_solution(3515067881126944736)
XLA Ops:
  0.6 307.6 %training_step.1 = (bf16[2,4,2,80,2048]{4,3,2,1,0:T(8,128)(2,1)}, bf16[2,4,2,80,2048]{4,3,2,1,0:T(8,128)(2,1)}, bf16[2,4,2,256,640]{4,3,2,1,0:T(8,128)(2,1)}, f3...) custom-call(bf16[2048,640]{1,0:T(8,128)(2,1)} %bitcast.8, ...), custom_call_target="tpu_custom_call" | custom-call | tf_op jit(solution)/shard_map/training_step/pallas_call | solution.py:718
  308.3 16.6 %results.1 = (bf16[2,640,2048]{2,1,0:T(8,128)(2,1)}, bf16[2,640,2048]{2,1,0:T(8,128)(2,1)}, bf16[2,2048,640]{2,1,0:T(8,128)(2,1)}, f32[2,80,2048]{2,1,0:T(8,128)...) custom-call(bf16[2,640,2048]{2,1,0:T(8,128)(2,1)} %bitcast.5, ...), custom_call_target="tpu_custom_call" | custom-call | tf_op jit(solution)/shard_map/results/pallas_call | solution.py:700

commit v4 on v3

--- a/solution.py
+++ b/solution.py
@@ -67,6 +67,9 @@
         value = (wide * scale_of(wide)).astype(BF16)
         a[at, :] = value
         a_t[:, at] = value.T
+
+    def load_tile(t):
+        return pltpu.make_async_copy(x_hbm.at[tile(t)], h.at[tile(t)], in_sem.at[2 + t])
 
     load_x = pltpu.make_async_copy(x_hbm, h, in_sem.at[0])
     load_dy = pltpu.make_async_copy(dy_hbm, d, in_sem.at[1])
@@ -163,12 +166,11 @@
         value = (d[at, :].astype(F32) + by_h.astype(BF16).astype(F32)).astype(BF16)
         d[at, :] = value
         d_t[:, at] = value.T
-
-    load_x.start()
-    load_x.wait()
+        load_tile(t).start()
 
     @pl.loop(0, TOKENS // T)
     def _(t):
+        load_tile(t).wait()
         norm_tile(tile(t), h[tile(t), :].astype(F32))
 
     backward(0)
@@ -187,7 +189,7 @@
     pltpu.VMEM((2, D, CH), BF16),
     pltpu.VMEM((2, D, CH), BF16),
     pltpu.VMEM((2, CH, D), BF16),
-    pltpu.SemaphoreType.DMA((2,)),
+    pltpu.SemaphoreType.DMA((2 + TOKENS // T,)),
     pltpu.SemaphoreType.DMA((2, 3)),
 ]
 
@@ -477,10 +479,6 @@
     pass_out(7)
     finish(6)
     finish(7)
-
-    @pl.loop(0, UNITS)
-    def _(u):
-        sent(u)
 
     norms[me] = squares[...]
 
@@ -571,6 +569,12 @@
         return pass_on(i, block, 2, device(z, 1 - k), k, src)
 
     for s in range(N + 3):
+        if s == 3:
+
+            @pl.loop(0, UNITS)
+            def _(u):
+                sent(u)
+
         if s < N:
             before = {2: 1, 4: 2, 5: 4}.get(s)
             if before is not None:
@@ -681,7 +685,7 @@
     def each(sem, sources, targets):
         return [
             pltpu.make_async_copy(sources[n].at[layer], targets[n].at[layer], sem.at[n, layer])
-            for n in range(9)
+            for n in (3, 4, 5, 0, 1, 2, 6, 7, 8)
             for layer in range(2)
         ]
 

time: 325 us -> 325 us (level)
  no operation moved by 1% of the time
where the time goes in v4:
time: 325 us; the launch traced here: 324 us
  Pallas kernels  324 us (100%)
    pallas_call x1, Pallas kernels, step(): pl.pallas_call(functools.partial(step_kernel, count), out_shape=[jax.Shap...  307 us
    pallas_call x1, Pallas kernels, copied(): pl.pallas_call(copy_kernel, out_shape=[jax.ShapeDtypeStruct(t.shape, t.dt...  16.4 us

profile of v4, /device:TPU:0, one launch (start us, length us, event | category | flops | bytes accessed | tf_op | source)
XLA Modules:
  0.0 324.4 jit_solution(7855707490930056566)
XLA Ops:
  0.6 307.2 %training_step.1 = (bf16[2,4,2,80,2048]{4,3,2,1,0:T(8,128)(2,1)}, bf16[2,4,2,80,2048]{4,3,2,1,0:T(8,128)(2,1)}, bf16[2,4,2,256,640]{4,3,2,1,0:T(8,128)(2,1)}, f3...) custom-call(bf16[2048,640]{1,0:T(8,128)(2,1)} %bitcast.8, ...), custom_call_target="tpu_custom_call" | custom-call | tf_op jit(solution)/shard_map/training_step/pallas_call | solution.py:722
  307.8 16.4 %results.1 = (bf16[2,640,2048]{2,1,0:T(8,128)(2,1)}, bf16[2,640,2048]{2,1,0:T(8,128)(2,1)}, bf16[2,2048,640]{2,1,0:T(8,128)(2,1)}, f32[2,80,2048]{2,1,0:T(8,128)...) custom-call(bf16[2,640,2048]{2,1,0:T(8,128)(2,1)} %bitcast.5, ...), custom_call_target="tpu_custom_call" | custom-call | tf_op jit(solution)/shard_map/results/pallas_call | solution.py:704
